TPU v7x, 256 devices: a whole 4x4x8 slice. The times are simulated.
256 devices in a mesh: section: 4 (over x_hi, core), dp: 64 (over y, x_lo, z).
Axes of the slice: x: 4 (x_hi: 2, x_lo: 2; x = x_hi * 2 + x_lo), y: 4, z: 8, core: 2. Of those that a mesh axis runs over, the one named last changes fastest.
Arguments:
- activations: bfloat16 [12288, 8, 4096], P('dp', 'section'), may hold values from -8 to 8
- damping: float32 [8], P('section'), may hold values from 0.1 to 1
Outputs:
- schur_inverse: float32 [256, 128, 128], P(('section', 'dp'))
- coupling: float32 [256, 128, 128], P(('section', 'dp'))
All inputs are finite; a program needn't handle non-finite values.
Results may differ from a plain program's by a relative error of at most 0.0003.
Values may be sent and summed in bfloat16 or wider, within the bound.
No kernel may reach another device: no remote copies, remote signals or barrier semaphores. Data moves between devices by JAX's collectives and lax.ppermute only.
A program may use at most 64 MiB of HBM per device.

v0:
```python
import jax
import jax.numpy as jnp
from jax import lax
from jax.sharding import PartitionSpec as P

B = 128


def passed_along(block, axis, distance):
    devices = range(lax.axis_size(axis))
    route = [(i - distance, i) for i in devices if i - distance in devices]
    return lax.ppermute(block, axis, route)


def sent_to_all(array, axis):
    copies = jnp.broadcast_to(array, (lax.axis_size(axis), *array.shape))
    return lax.all_to_all(copies, axis, split_axis=0, concat_axis=0, tiled=True)


def over_copies(array, axis):
    everything = sent_to_all(array, axis)
    return jnp.sum(everything, axis=0)


def solve_block(system, right_side):
    factor = jnp.linalg.cholesky(system)
    return jax.scipy.linalg.cho_solve((factor, True), right_side)


def local(activations, damping):
    token_rows, local_layers, model_width = activations.shape
    block_size = B
    blocks_layer = model_width // block_size
    group_size = lax.axis_size("dp")
    section_count = lax.axis_size("section")
    per_device = local_layers * blocks_layer // group_size
    tokens_all = token_rows * group_size
    flattened = activations.reshape(token_rows, local_layers * model_width)
    following_rows = passed_along(flattened[:, :model_width], "section", -1)
    next_layers = jnp.concatenate([flattened[:, model_width:], following_rows], axis=1)
    owner_layer = lax.axis_index("dp") * per_device // blocks_layer
    layer_index = jnp.arange(local_layers)
    sent_pairs = (
        flattened.reshape(token_rows, group_size, per_device * block_size),
        next_layers.reshape(token_rows, group_size, per_device * block_size),
    )
    left_cols, right_cols = (
        lax.all_to_all(sent_pairs[0], "dp", split_axis=1, concat_axis=0, tiled=True),
        lax.all_to_all(sent_pairs[1], "dp", split_axis=1, concat_axis=0, tiled=True),
    )
    diagonal_gram = (
        jnp.einsum("tgb,tgc->gbc", left_cols, left_cols, preferred_element_type=jnp.float32)
        / tokens_all
    )
    cross_gram = (
        jnp.einsum("tgb,tgc->gbc", left_cols, right_cols, preferred_element_type=jnp.float32)
        / tokens_all
    )
    owned_trace = jnp.sum(jnp.trace(diagonal_gram, axis1=1, axis2=2))
    traces = over_copies(jnp.where(layer_index == owner_layer, owned_trace, 0.0), "dp")
    identity = jnp.eye(block_size, dtype=jnp.float32)
    damp_level = jnp.sum(jnp.where(layer_index == owner_layer, traces * damping, 0.0)) / model_width
    damped = diagonal_gram + damp_level * identity
    following_damped = passed_along(damped, ("section", "dp"), -(group_size // local_layers))
    final_layer = jnp.logical_and(
        lax.axis_index("section") == section_count - 1, owner_layer == local_layers - 1
    )
    system = jnp.where(final_layer, identity, following_damped)
    cross_gram = jnp.where(final_layer, jnp.zeros_like(cross_gram), cross_gram)
    coupling_t = jax.vmap(solve_block)(system, jnp.swapaxes(cross_gram, 1, 2))
    schur = damped - jnp.matmul(cross_gram, coupling_t, precision=lax.Precision.HIGHEST)
    identities = jnp.broadcast_to(identity, schur.shape)
    schur_inverse = jax.vmap(solve_block)(schur, identities)
    return (schur_inverse, jnp.swapaxes(coupling_t, 1, 2))


def solution(mesh):
    placed = (P("dp", "section", None), P("section"))
    return jax.shard_map(
        local,
        mesh=mesh,
        in_specs=placed,
        out_specs=(P(("section", "dp"), None, None), P(("section", "dp"), None, None)),
        check_vma=False,
    )
```

profile of v0, /device:TPU:1, one launch (start us, length us, event | category | flops | bytes accessed | tf_op | source)
XLA Modules:
  0.0 221.7 jit_solution(8540265799306868774)
XLA Ops:
  0.6 4.8 %reshape_reshape.3 = bf16[192,64,128]{2,1,0:T(8,128)(2,1)S(1)} reshape(bf16[192,2,4096]{2,1,0:T(2,128)(2,1)} %param.5) | data formatting | bytes 6291456 | tf_op jit(solution)/shard_map/reshape;reshape | solution.py:44
  5.4 3.7 %copy.26 = bf16[192,64,128]{2,0,1:T(8,128)(2,1)} copy(bf16[192,64,128]{2,1,0:T(8,128)(2,1)S(1)} %reshape_reshape.3) | data formatting | bytes 6291456 | tf_op jit(solution)/shard_map/reshape;reshape | solution.py:44
  9.2 0.0 copy-start
  9.2 14.1 %all-to-all-start = ((bf16[192,64,128]{2,0,1:T(8,128)(2,1)}), bf16[192,64,128]{2,0,1:T(8,128)(2,1)}, u32[]{:S(2)}, u32[]{:S(2)}) async-start(bf16[192,64,128]{2,0,1:T(8,128)(2,1)} %copy.26), calls=%async_computation | async-start | bytes 6291456 | tf_op jit(solution)/shard_map/all_to_all | solution.py:48
  23.2 0.0 copy-done
  23.3 2.1 copy.42
  25.3 0.2 fusion.41
  25.6 2.9 %collective-permute-start = (bf16[192,4096]{1,0:T(8,128)(2,1)S(1)}, bf16[192,4096]{1,0:T(8,128)(2,1)}, u32[]{:S(2)}, u32[]{:S(2)}) collective-permute-start(bf16[192,4096]{1,0:T(8,128)(2,1)S(1)} %get-tuple-element.13), channel_id=1, source_target_pairs={{64,0},{128,64},{192,128},{65,1},{129,65},{193,129},{66,2},{130,66... | collective-permute-start | bytes 4718600 | tf_op jit(solution)/shard_map/ppermute | solution.py:12
  28.4 63.7 %all-to-all-done = bf16[192,64,128]{2,0,1:T(8,128)(2,1)} async-done(((bf16[192,64,128]{2,0,1:T(8,128)(2,1)}), bf16[192,64,128]{2,0,1:T(8,128)(2,1)}, u32[]{:S(2)}, u32[]{:S(2)}) %all-to-all-start) | async-done | bytes 3145760 | tf_op jit(solution)/shard_map/all_to_all | solution.py:48
  92.2 4.5 %select_reduce_fusion.1 = (f32[]{:T(128)}, f32[128,128]{0,1:T(8,128)S(1)}) fusion(bf16[192,64,128]{2,0,1:T(8,128)(2,1)} %all-to-all-done), kind=kOutput, calls=%fused_computation.38 | convolution fusion | flops 402718720 | bytes 3211268 | tf_op jit(solution)/shard_map/tgb,tgc->gbc/dot_general | solution.py:52
  96.7 0.6 compare_select_fusion.1
  97.3 0.6 broadcast_in_dim.31
  98.0 10.7 %all-to-all-start.1 = ((f32[64,1,2]{2,1,0:T(1,128)}), f32[64,1,2]{2,1,0:T(1,128)S(1)}, u32[]{:S(2)}, u32[]{:S(2)}) async-start(f32[64,1,2]{2,1,0:T(1,128)} %broadcast_in_dim.31), calls=%async_computation.1 | async-start | bytes 65536 | tf_op jit(solution)/shard_map/all_to_all | solution.py:17
  108.6 0.0 collective-permute-done
  108.7 4.0 %copy_bitcast_fusion = bf16[192,64,128]{2,0,1:T(8,128)(2,1)} fusion(bf16[192,4096]{1,0:T(8,128)(2,1)} %collective-permute-done, bf16[192,4096]{1,0:T(8,128)(2,1)S(1)} %get-tuple-element.12), kind=kLoop, calls=%fused_computation | loop fusion | flops 6291456 | bytes 6291456 | tf_op jit(solution)/shard_map/reshape | solution.py:45
  112.7 0.0 copy-start.1
  112.7 5.2 %all-to-all-done.1 = f32[64,1,2]{2,1,0:T(1,128)S(1)} async-done(((f32[64,1,2]{2,1,0:T(1,128)}), f32[64,1,2]{2,1,0:T(1,128)S(1)}, u32[]{:S(2)}, u32[]{:S(2)}) %all-to-all-start.1) | async-done | bytes 544 | tf_op jit(solution)/shard_map/all_to_all | solution.py:17
  117.9 5.6 %all-to-all-start.2 = ((bf16[192,64,128]{2,0,1:T(8,128)(2,1)}), bf16[192,64,128]{2,0,1:T(8,128)(2,1)S(1)}, u32[]{:S(2)}, u32[]{:S(2)}) async-start(bf16[192,64,128]{2,0,1:T(8,128)(2,1)} %copy_bitcast_fusion), calls=%async_computation.2 | async-start | bytes 6291456 | tf_op jit(solution)/shard_map/all_to_all | solution.py:49
  123.5 0.1 reduce_sum.33
  123.6 0.0 copy-done.1
  123.6 0.6 fusion.40
  124.9 6.6 %collective-permute-start.1 = (f32[1,128,128]{1,2,0:T(8,128)S(1)}, f32[1,128,128]{1,2,0:T(8,128)S(1)}, u32[]{:S(2)}, u32[]{:S(2)}) collective-permute-start(f32[1,128,128]{1,2,0:T(8,128)S(1)} %fusion.39), channel_id=1, source_target_pairs={{32,0},{33,1},{34,2},{35,3},{36,4},{37,5},{38,6},{39,7},{40,8},{41... | collective-permute-start | bytes 196616 | tf_op jit(solution)/shard_map/ppermute | solution.py:12
  131.5 1.6 collective-permute-done.1
  133.1 0.1 copy.31
  133.2 11.7 %custom-call.10 = f32[1,128,128]{2,1,0:T(8,128)S(1)} custom-call(f32[1,128,128]{2,1,0:T(8,128)S(1)} %fusion.36), custom_call_target="Cholesky" | custom-call | tf_op jit(solution)/shard_map/vmap(jit(cholesky))/cholesky | solution.py:26
  144.9 0.6 compare_reduce_fusion.1
  145.6 0.7 fusion.26
  146.2 9.8 %custom-call.11 = f32[1,1,128,128]{2,3,1,0:T(8,128)S(1)} custom-call(f32[1,1,128,128]{3,2,1,0:T(8,128)S(1)} %fusion.26), custom_call_target="InvertDiagBlocksLowerTriangular" | custom-call | tf_op jit(solution)/shard_map/vmap(jit(_cho_solve))/triangular_solve | solution.py:27
  156.1 37.0 %all-to-all-done.2 = bf16[192,64,128]{2,0,1:T(8,128)(2,1)S(1)} async-done(((bf16[192,64,128]{2,0,1:T(8,128)(2,1)}), bf16[192,64,128]{2,0,1:T(8,128)(2,1)S(1)}, u32[]{:S(2)}, u32[]{:S(2)}) %all-to-all-start.2) | async-done | bytes 3145760 | tf_op jit(solution)/shard_map/all_to_all | solution.py:49
  193.0 3.0 %fusion.21 = f32[128,128]{0,1:T(8,128)S(1)} fusion(bf16[192,64,128]{2,0,1:T(8,128)(2,1)} %all-to-all-done, bf16[192,64,128]{2,0,1:T(8,128)(2,1)S(1)} %all-to-all-done.2, pred[]{:T(512)S(6)} %and.11), kind=kOutput, calls=%fused_computation.13 | convolution fusion | flops 402685952 | bytes 6356993 | tf_op jit(solution)/shard_map/tgb,tgc->gbc/dot_general | solution.py:56
  196.0 0.3 fusion.34
  196.3 0.2 fusion.32
  196.5 0.3 convolution_subtract_fusion
  196.8 0.1 copy.33
  196.9 11.7 %custom-call.12 = f32[1,128,128]{2,1,0:T(8,128)S(1)} custom-call(f32[1,128,128]{2,1,0:T(8,128)S(1)} %fusion.29), custom_call_target="Cholesky" | custom-call | tf_op jit(solution)/shard_map/vmap(jit(cholesky))/cholesky | solution.py:26
  208.7 0.6 compare_reduce_fusion
  209.3 0.7 fusion.27
  210.0 9.8 %custom-call.13 = f32[1,1,128,128]{2,3,1,0:T(8,128)S(1)} custom-call(f32[1,1,128,128]{3,2,1,0:T(8,128)S(1)} %fusion.27), custom_call_target="InvertDiagBlocksLowerTriangular" | custom-call | tf_op jit(solution)/shard_map/vmap(jit(_cho_solve))/triangular_solve | solution.py:27
  219.8 0.3 fusion.28
  220.1 0.8 convolution_bitcast_fusion
  220.9 0.7 copy.34
  (6 shorter events, 0.1 us)
Async XLA Ops:
  9.2 14.1 %copy-start = (bf16[192,2,4096]{2,1,0:T(2,128)(2,1)S(1)}, bf16[192,2,4096]{2,1,0:T(2,128)(2,1)}, u32[]{:S(2)}) copy-start(bf16[192,2,4096]{2,1,0:T(2,128)(2,1)} %param.5) | copy-start | bytes 9437188
  9.2 83.0 %all-to-all-start = ((bf16[192,64,128]{2,0,1:T(8,128)(2,1)}), bf16[192,64,128]{2,0,1:T(8,128)(2,1)}, u32[]{:S(2)}, u32[]{:S(2)}) async-start(bf16[192,64,128]{2,0,1:T(8,128)(2,1)} %copy.26), calls=%async_computation | async-start | bytes 6291456 | tf_op jit(solution)/shard_map/all_to_all | solution.py:48
  25.6 83.1 %collective-permute-start = (bf16[192,4096]{1,0:T(8,128)(2,1)S(1)}, bf16[192,4096]{1,0:T(8,128)(2,1)}, u32[]{:S(2)}, u32[]{:S(2)}) collective-permute-start(bf16[192,4096]{1,0:T(8,128)(2,1)S(1)} %get-tuple-element.13), channel_id=1, source_target_pairs={{64,0},{128,64},{192,128},{65,1},{129,65},{193,129},{66,2},{130,66... | collective-permute-start | bytes 4718600 | tf_op jit(solution)/shard_map/ppermute | solution.py:12
  98.0 19.9 %all-to-all-start.1 = ((f32[64,1,2]{2,1,0:T(1,128)}), f32[64,1,2]{2,1,0:T(1,128)S(1)}, u32[]{:S(2)}, u32[]{:S(2)}) async-start(f32[64,1,2]{2,1,0:T(1,128)} %broadcast_in_dim.31), calls=%async_computation.1 | async-start | bytes 65536 | tf_op jit(solution)/shard_map/all_to_all | solution.py:17
  112.7 10.9 %copy-start.1 = (f32[2]{0:T(128)S(1)}, f32[2]{0:T(128)}, u32[]{:S(2)}) copy-start(f32[2]{0:T(128)} %param.6) | copy-start | bytes 28
  117.9 75.2 %all-to-all-start.2 = ((bf16[192,64,128]{2,0,1:T(8,128)(2,1)}), bf16[192,64,128]{2,0,1:T(8,128)(2,1)S(1)}, u32[]{:S(2)}, u32[]{:S(2)}) async-start(bf16[192,64,128]{2,0,1:T(8,128)(2,1)} %copy_bitcast_fusion), calls=%async_computation.2 | async-start | bytes 6291456 | tf_op jit(solution)/shard_map/all_to_all | solution.py:49
  124.9 8.2 %collective-permute-start.1 = (f32[1,128,128]{1,2,0:T(8,128)S(1)}, f32[1,128,128]{1,2,0:T(8,128)S(1)}, u32[]{:S(2)}, u32[]{:S(2)}) collective-permute-start(f32[1,128,128]{1,2,0:T(8,128)S(1)} %fusion.39), channel_id=1, source_target_pairs={{32,0},{33,1},{34,2},{35,3},{36,4},{37,5},{38,6},{39,7},{40,8},{41... | collective-permute-start | bytes 196616 | tf_op jit(solution)/shard_map/ppermute | solution.py:12
where the time goes:
time: 225 us; the launch traced here: 222 us
  waiting for transfers between devices  108 us (48%)
  other arithmetic  51.1 us (23%)
  starting transfers between devices  39.8 us (18%)
  local copies, waits for them, and re-layouts  12.4 us (6%)
  matrix products  9.38 us (4%)
    all_to_all x1, waiting for transfers between devices, local(): lax.all_to_all(sent_pairs[0], 'dp', split_axis=1, concat_axis=0, tiled=True)  63.7 us
    all_to_all x1, waiting for transfers between devices, local(): lax.all_to_all(sent_pairs[1], 'dp', split_axis=1, concat_axis=0, tiled=True)  37 us
    another operation x6, other arithmetic, solve_block(): factor = jnp.linalg.cholesky(system)  24.8 us
    another operation x4, other arithmetic, solve_block(): return jax.scipy.linalg.cho_solve((factor, True), right_side)  20.9 us
    all_to_all x1, starting transfers between devices, local(): lax.all_to_all(sent_pairs[0], 'dp', split_axis=1, concat_axis=0, tiled=True)  14.1 us
    all_to_all x1, starting transfers between devices, sent_to_all(): return lax.all_to_all(copies, axis, split_axis=0, concat_axis=0, tiled=True)  10.7 us
    ppermute x2, starting transfers between devices, passed_along(): return lax.ppermute(block, axis, route)  9.45 us
    another operation x2, local copies, waits for them, and re-layouts, local(): flattened.reshape(token_rows, group_size, per_device * block_size)  8.53 us
  transfers between devices with their start and end apart: 5, of which 4 were waited for; matrix products, arithmetic and copies ran while one was open for 16% of the time, Pallas kernels for 0%

commit v1 on v0

v1 whole, which is shorter than its diff:
```python
from functools import partial

import jax
import jax.numpy as jnp
from jax import lax
from jax.experimental import pallas as pl
from jax.experimental.pallas import tpu as pltpu
from jax.sharding import PartitionSpec as P

B = 128
EVERY = ("section", "dp")


def dp_index(y1, y0, xl, z2, z1, z0):
    return ((((y1 * 2 + y0) * 2 + xl) * 2 + z2) * 2 + z1) * 2 + z0


def flipped(section):
    return section // 2


BITS = [tuple((d >> s) & 1 for s in (5, 4, 3, 2, 1, 0)) for d in range(64)]


def column_groups():
    groups = []
    for section in range(4):
        for z2 in range(2):
            for z1 in range(2):
                groups.append(
                    [
                        section * 64 + dp_index(m >> 3, (m >> 2) & 1, ((m >> 1) & 1) ^ flipped(section), z2, z1, m & 1)
                        for m in range(16)
                    ]
                )
    return groups


def following_route():
    route = []
    for section in range(1, 4):
        turn = flipped(section) ^ flipped(section - 1)
        for d, (y1, y0, xl, z2, z1, z0) in enumerate(BITS):
            route.append((section * 64 + d, (section - 1) * 64 + dp_index(y1, y0, xl ^ turn, z2, z1, z0)))
    return route


def home_route(a, b):
    route = []
    for section in range(4):
        turn = flipped(section)
        for d, (y1, y0, xl, z2, z1, z0) in enumerate(BITS):
            route.append((section * 64 + d, section * 64 + dp_index(z1 ^ a, y0, xl ^ turn, z2 ^ b, y1, z0)))
    return route


def gram_kernel(pos_ref, x0_ref, x1_ref, x2_ref, *out_refs):
    turn, z2, z1 = pos_ref[0], pos_ref[1], pos_ref[2]
    chunks, rows, _ = x0_ref.shape
    row = lax.broadcasted_iota(jnp.int32, (B, B), 0)
    col = lax.broadcasted_iota(jnp.int32, (B, B), 1)
    dims = (((0,), (0,)), ((), ()))
    half = chunks // 2

    def gram(left, right):
        return lax.dot_general(left, right, dims, preferred_element_type=jnp.float32)

    for zz in range(2):
        cols = pl.ds(zz * B, B)
        totals = [jnp.zeros((B, B), jnp.float32) for _ in range(5)]
        for j in range(chunks):
            x0 = x0_ref[j, :, cols]
            x1 = x1_ref[j, :, cols]
            x2 = x2_ref[j ^ (turn * 2), :, cols]
            for i, (p, q) in enumerate(((x0, x0), (x1, x1), (x2, x2), (x0, x1), (x1, x2))):
                totals[i] = totals[i] + gram(p, q)
        d0, d1, d2, c01, c12 = totals
        for layer, (d, n, c) in enumerate(((d0, d1, c01), (d1, d2, c12))):
            packed = jnp.where(row >= col, d, n)
            edge = jnp.sum(jnp.where(row == col, n, 0.0), axis=0, keepdims=True)
            edge = jnp.broadcast_to(edge, (8, B))
            for b in range(2):
                for a in range(2):

                    @pl.when(jnp.logical_and((z2 ^ b) == zz, (z1 ^ a) == layer))
                    def _():
                        out = out_refs[a * 2 + b]
                        out[0:B, :] = c
                        out[B : 2 * B, :] = packed
                        out[2 * B : 2 * B + 8, :] = edge


def partial_grams(x0, x1, x2, position):
    vmem = pl.BlockSpec(memory_space=pltpu.VMEM)
    return pl.pallas_call(
        gram_kernel,
        out_shape=[jax.ShapeDtypeStruct((2 * B + 8, B), jnp.float32)] * 4,
        in_specs=[pl.BlockSpec(memory_space=pltpu.SMEM), vmem, vmem, vmem],
        out_specs=[vmem] * 4,
        name="partial_grams",
        cost_estimate=pl.CostEstimate(flops=10 * 3072 * B * B * 2, bytes_accessed=6 * 3072 * B * 2, transcendentals=0),
        compiler_params=pltpu.CompilerParams(vmem_limit_bytes=24 * 2**20),
    )(position, x0, x1, x2)


def solve_block(system, right_side):
    factor = jnp.linalg.cholesky(system)
    return jax.scipy.linalg.cho_solve((factor, True), right_side)


def local(activations, damping):
    token_rows, local_layers, model_width = activations.shape
    group_size = lax.axis_size("dp")
    section_count = lax.axis_size("section")
    tokens_all = token_rows * group_size
    section = lax.axis_index("section")
    dp = lax.axis_index("dp")
    owner_layer = dp // 32
    z2, z1 = (dp >> 2) & 1, (dp >> 1) & 1
    groups = column_groups()

    def by_member(layer):
        cut = activations[:, layer, :].reshape(token_rows, 2, 2, 2, 2, 2, B)
        return cut.transpose(4, 1, 2, 5, 0, 3, 6).reshape(16, token_rows, 2 * B)

    def exchanged(columns):
        return lax.all_to_all(columns, EVERY, split_axis=0, concat_axis=0, axis_index_groups=groups, tiled=True)

    x0 = exchanged(by_member(0))
    squares = jnp.sum(jnp.square(activations.astype(jnp.float32)), axis=(0, 2))
    copies = jnp.broadcast_to(squares, (group_size, 1, local_layers))
    squares = lax.all_to_all(copies, "dp", split_axis=0, concat_axis=0, tiled=True)
    levels = damping * (jnp.sum(squares, axis=(0, 1)) / tokens_all) / model_width
    next_level = lax.ppermute(levels, "section", [(i, i - 1) for i in range(1, section_count)])
    x2 = lax.ppermute(x0, EVERY, following_route())
    x1 = exchanged(by_member(1))
    position = jnp.stack([(section == 1).astype(jnp.int32), z2.astype(jnp.int32), z1.astype(jnp.int32)])
    sent = partial_grams(x0, x1, x2, position)
    arrived = [lax.ppermute(sent[a * 2 + b], EVERY, home_route(a, b)) for a in range(2) for b in range(2)]
    owned = sum(arrived[1:], arrived[0]) / tokens_all

    identity = jnp.eye(B, dtype=jnp.float32)
    cross_gram, packed, edge = owned[:B], owned[B : 2 * B], owned[2 * B]
    lower = jnp.tril(packed, -1)
    upper = jnp.triu(packed, 1)
    level = jnp.where(owner_layer == 0, levels[0], levels[1])
    level_after = jnp.where(owner_layer == 0, levels[1], next_level[0])
    damped = lower + lower.T + packed * identity + level * identity
    following = upper + upper.T + edge[:, None] * identity + level_after * identity
    final_layer = jnp.logical_and(section == section_count - 1, owner_layer == local_layers - 1)
    system = jnp.where(final_layer, identity, following)
    cross_gram = jnp.where(final_layer, jnp.zeros_like(cross_gram), cross_gram)
    coupling_t = solve_block(system, cross_gram.T)
    schur = damped - jnp.matmul(cross_gram, coupling_t, precision=lax.Precision.HIGHEST)
    schur_inverse = solve_block(schur, identity)
    return (schur_inverse[None], coupling_t.T[None])


def solution(mesh):
    placed = (P("dp", "section", None), P("section"))
    return jax.shard_map(
        local,
        mesh=mesh,
        in_specs=placed,
        out_specs=(P(("section", "dp"), None, None), P(("section", "dp"), None, None)),
        check_vma=False,
    )
```

time: 225 us -> 187 us (0.83); the launches traced: 222 us -> 187 us
  waiting for transfers between devices: 108 us -> 43.2 us
  local copies, waits for them, and re-layouts: 12.4 us -> 33.8 us
  Pallas kernels: 0 us -> 8.02 us
  matrix products: 9.38 us -> 1.9 us
  other arithmetic: 51.1 us -> 56.9 us
    all_to_all x3, waiting for transfers between devices: 106 us -> 25.5 us  [the longest x2 25.5 us: exchanged(): lax.all_to_all(columns, EVERY, split_axis=0, concat_axis=0, axis_index_gr...]
    slice x1 -> x4, local copies, waits for them, and re-layouts: 0.2 us -> 16.8 us  [the longest x1 16.1 us: by_member(): cut = activations[:, layer, :].reshape(token_rows, 2, 2, 2, 2, 2, B)]
    ppermute x2 -> x6, waiting for transfers between devices: 1.59 us -> 17.6 us  [the longest x1 13.1 us: local(): lax.ppermute(levels, 'section', [(i, i - 1) for i in range(1, section_cou...]
    reduce_sum x2, other arithmetic: 0.69 us -> 9.22 us  [the longest x1 8.62 us: local(): squares = jnp.sum(jnp.square(activations.astype(jnp.float32)), axis=(0, 2))]
    pallas_call x0 -> x1, Pallas kernels: none -> 8.02 us  [partial_grams(): pl.pallas_call(gram_kernel, out_shape=[jax.ShapeDtypeStruct((2 * B + 8, B...]
    dot_general x2 -> x0, matrix products: 7.48 us -> none  [the longest x1 4.5 us: local(): jnp.einsum('tgb,tgc->gbc', left_cols, left_cols, preferred_element_type=j...]
    ppermute x2 -> x6, starting transfers between devices: 9.45 us -> 15.7 us  [the longest x4 9.28 us: local(): lax.ppermute(sent[a * 2 + b], EVERY, home_route(a, b))]
    all_to_all x3, starting transfers between devices: 30.4 us -> 24.3 us  [the longest x1 13.8 us: local(): lax.all_to_all(copies, 'dp', split_axis=0, concat_axis=0, tiled=True)]
  transfers between devices with their start and end apart: 5 -> 9, of which waited for: 4 -> 4; matrix products, arithmetic and copies ran while one was open for 16% -> 18% of each run, Pallas kernels for 0% -> 0%
where the time goes in v1:
time: 187 us
  other arithmetic  56.9 us (30%)
  waiting for transfers between devices  43.2 us (23%)
  starting transfers between devices  40 us (21%)
  local copies, waits for them, and re-layouts  33.8 us (18%)
  Pallas kernels  8.02 us (4%)
  between operations  2.98 us (2%)
  matrix products  1.9 us (1%)
    all_to_all x2, waiting for transfers between devices, exchanged(): lax.all_to_all(columns, EVERY, split_axis=0, concat_axis=0, axis_index_gr...  25.5 us
    another operation x6, other arithmetic, solve_block(): factor = jnp.linalg.cholesky(system)  24.8 us
    another operation x4, other arithmetic, solve_block(): return jax.scipy.linalg.cho_solve((factor, True), right_side)  20.9 us
    slice x1, local copies, waits for them, and re-layouts, by_member(): cut = activations[:, layer, :].reshape(token_rows, 2, 2, 2, 2, 2, B)  16.1 us
    all_to_all x1, starting transfers between devices, local(): lax.all_to_all(copies, 'dp', split_axis=0, concat_axis=0, tiled=True)  13.8 us
    ppermute x1, waiting for transfers between devices, local(): lax.ppermute(levels, 'section', [(i, i - 1) for i in range(1, section_cou...  13.1 us
    all_to_all x2, starting transfers between devices, exchanged(): lax.all_to_all(columns, EVERY, split_axis=0, concat_axis=0, axis_index_gr...  10.6 us
    ppermute x4, starting transfers between devices, local(): lax.ppermute(sent[a * 2 + b], EVERY, home_route(a, b))  9.28 us
  transfers between devices with their start and end apart: 9, of which 4 were waited for; matrix products, arithmetic and copies ran while one was open for 18% of the time, Pallas kernels for 0%

profile of v1, /device:TPU:1, one launch (start us, length us, event | category | flops | bytes accessed | tf_op | source)
XLA Modules:
  0.0 186.8 jit_solution(15482440312721908052)
XLA Ops:
  0.6 8.6 %multiply_reduce_fusion = f32[2]{0:T(128)S(1)} fusion(bf16[192,2,4096]{2,1,0:T(2,128)(2,1)} %param.5), kind=kLoop, calls=%fused_computation | loop fusion | flops 4718590 | bytes 3145736 | tf_op jit(solution)/shard_map/reduce_sum | solution.py:130
  9.3 0.6 broadcast_in_dim.18
  9.9 13.8 %all-to-all-start.2 = ((f32[64,1,2]{2,1,0:T(1,128)}), f32[64,1,2]{2,1,0:T(1,128)S(1)}, u32[]{:S(2)}, u32[]{:S(2)}) async-start(f32[64,1,2]{2,1,0:T(1,128)} %broadcast_in_dim.18), calls=%async_computation.2 | async-start | bytes 65536 | tf_op jit(solution)/shard_map/all_to_all | solution.py:132
  23.7 16.1 %slice_reduce_fusion = (bf16[192,4096]{1,0:T(8,128)(2,1)}, bf16[192,4096]{1,0:T(8,128)(2,1)}) fusion(bf16[192,2,4096]{2,1,0:T(2,128)(2,1)S(1)} %copy-done), kind=kLoop, calls=%fused_computation.1 | loop fusion | bytes 6291456 | tf_op jit(solution)/shard_map/slice | solution.py:123
  39.7 2.8 %reshape_squeeze.6 = bf16[192,2,2,2,2,2,128]{6,5,4,3,2,1,0:T(2,128)(2,1)S(1)} reshape(bf16[192,4096]{1,0:T(8,128)(2,1)} %get-tuple-element.21) | data formatting | bytes 3145728 | tf_op jit(solution)/shard_map/reshape;squeeze | solution.py:123
  42.5 1.6 copy.49
  44.2 2.3 %reshape.21 = bf16[16,192,256]{2,1,0:T(8,128)(2,1)} reshape(bf16[2,2,2,2,192,2,128]{6,5,4,3,2,1,0:T(2,128)(2,1)S(1)} %copy.49) | data formatting | bytes 3145728 | tf_op jit(solution)/shard_map/reshape | solution.py:124
  46.5 5.8 %all-to-all-start = ((bf16[16,192,256]{2,1,0:T(8,128)(2,1)}), bf16[16,192,256]{2,1,0:T(8,128)(2,1)S(1)}, u32[]{:S(2)}, u32[]{:S(2)}) async-start(bf16[16,192,256]{2,1,0:T(8,128)(2,1)} %reshape.21), calls=%async_computation | async-start | bytes 3145728 | tf_op jit(solution)/shard_map/all_to_all | solution.py:127
  52.3 2.4 %reshape_squeeze.7 = bf16[192,2,2,2,2,2,128]{6,5,4,3,2,1,0:T(2,128)(2,1)} reshape(bf16[192,4096]{1,0:T(8,128)(2,1)S(1)} %copy-done.1) | data formatting | bytes 3145728 | tf_op jit(solution)/shard_map/reshape;squeeze | solution.py:123
  54.7 3.0 %copy.50 = bf16[2,2,2,2,192,2,128]{6,5,4,3,2,1,0:T(2,128)(2,1)S(1)} copy(bf16[2,2,2,2,192,2,128]{6,3,0,5,2,1,4:T(2,128)(2,1)} %bitcast.57) | data formatting | bytes 3145728 | tf_op jit(solution)/shard_map/transpose | solution.py:124
  57.7 2.3 %reshape.22 = bf16[16,192,256]{2,1,0:T(8,128)(2,1)} reshape(bf16[2,2,2,2,192,2,128]{6,5,4,3,2,1,0:T(2,128)(2,1)S(1)} %copy.50) | data formatting | bytes 3145728 | tf_op jit(solution)/shard_map/reshape | solution.py:124
  60.0 12.4 %all-to-all-done.x0_ref = bf16[16,192,256]{2,1,0:T(8,128)(2,1)S(1)} async-done(((bf16[16,192,256]{2,1,0:T(8,128)(2,1)}), bf16[16,192,256]{2,1,0:T(8,128)(2,1)S(1)}, u32[]{:S(2)}, u32[]{:S(2)}) %all-to-all-start) | async-done | bytes 1572896 | tf_op jit(solution)/shard_map/all_to_all | solution.py:127
  72.4 4.7 %all-to-all-start.1 = ((bf16[16,192,256]{2,1,0:T(8,128)(2,1)}), bf16[16,192,256]{2,1,0:T(8,128)(2,1)S(1)}, u32[]{:S(2)}, u32[]{:S(2)}) async-start(bf16[16,192,256]{2,1,0:T(8,128)(2,1)} %reshape.22), calls=%async_computation.1 | async-start | bytes 3145728 | tf_op jit(solution)/shard_map/all_to_all | solution.py:127
  77.2 4.3 %collective-permute-start = (bf16[16,192,256]{2,1,0:T(8,128)(2,1)S(1)}, bf16[16,192,256]{2,1,0:T(8,128)(2,1)}, u32[]{:S(2)}, u32[]{:S(2)}) collective-permute-start(bf16[16,192,256]{2,1,0:T(8,128)(2,1)S(1)} %all-to-all-done.x0_ref), channel_id=1, source_target_pairs={{64,0},{65,1},{66,2},{67,3},{68,4},{69,5},{70,6},{71,7},{72,8},{73... | collective-permute-start | bytes 4718600 | tf_op jit(solution)/shard_map/ppermute | solution.py:135
  81.5 0.7 copy.53
  82.2 0.5 iota_add_fusion
  82.8 0.6 reduce_sum.19
  83.4 13.1 %all-to-all-done.1.x1_ref = bf16[16,192,256]{2,1,0:T(8,128)(2,1)S(1)} async-done(((bf16[16,192,256]{2,1,0:T(8,128)(2,1)}), bf16[16,192,256]{2,1,0:T(8,128)(2,1)S(1)}, u32[]{:S(2)}, u32[]{:S(2)}) %all-to-all-start.1) | async-done | bytes 1572896 | tf_op jit(solution)/shard_map/all_to_all | solution.py:127
  96.5 4.6 %collective-permute-done.x2_ref = bf16[16,192,256]{2,1,0:T(8,128)(2,1)} collective-permute-done((bf16[16,192,256]{2,1,0:T(8,128)(2,1)S(1)}, bf16[16,192,256]{2,1,0:T(8,128)(2,1)}, u32[]{:S(2)}, u32[]{:S(2)}) %collective-permute-start) | collective-permute-done | bytes 1572896 | tf_op jit(solution)/shard_map/ppermute | solution.py:135
  101.1 8.0 %partial_grams.1 = (f32[264,128]{1,0:T(8,128)S(1)}, f32[264,128]{1,0:T(8,128)S(1)}, f32[264,128]{1,0:T(8,128)S(1)}, f32[264,128]{1,0:T(8,128)}) custom-call(s32[3]{0:T(128)S(1)} %pad_add_fusion.pos_ref, bf16[16,192,256]{2,1,0:T(8,128)(2,1)S(1)} %all-to-all-done.x0_ref, bf16[16,192,256]{2,1,0:T(8,128)(2,1)S(1)} %all-to-all-done.1.x1_ref, ...), custom_call_target="tpu_custom_call" | custom-call | flops 1006632960 | bytes 4718592 | tf_op jit(solution)/shard_map/partial_grams/pallas_call | solution.py:95
  109.1 7.1 %collective-permute-start.4 = (f32[264,128]{1,0:T(8,128)}, f32[264,128]{1,0:T(8,128)S(1)}, u32[]{:S(2)}, u32[]{:S(2)}) collective-permute-start(f32[264,128]{1,0:T(8,128)} %get-tuple-element.11), channel_id=1, source_target_pairs={{0,36},{1,37},{2,4},{3,5},{4,32},{5,33},{6,0},{7,1},{8,44},{9,45},... | collective-permute-start | bytes 405512 | tf_op jit(solution)/shard_map/ppermute | solution.py:139
  116.2 0.7 collective-permute-start.1
  116.9 1.5 collective-permute-start.2
  118.4 2.1 %collective-permute-start.5 = (f32[2]{0:T(128)S(1)}, f32[2]{0:T(128)S(1)}, u32[]{:S(2)}, u32[]{:S(2)}) collective-permute-start(f32[2]{0:T(128)S(1)} %multiply_multiply_fusion), channel_id=1, source_target_pairs={{64,0},{128,64},{192,128},{65,1},{129,65},{193,129},{66,2},{130,66... | collective-permute-start | bytes 32 | tf_op jit(solution)/shard_map/ppermute | solution.py:134
  120.6 0.7 fusion.26
  122.6 13.1 %collective-permute-done.5 = f32[2]{0:T(128)S(1)} collective-permute-done((f32[2]{0:T(128)S(1)}, f32[2]{0:T(128)S(1)}, u32[]{:S(2)}, u32[]{:S(2)}) %collective-permute-start.5) | collective-permute-done | bytes 40 | tf_op jit(solution)/shard_map/ppermute | solution.py:134
  136.4 0.1 copy.51
  136.5 0.6 fusion.19
  137.1 0.1 copy.52
  137.2 0.8 fusion.15
  138.0 0.1 copy.59
  138.1 0.1 copy.61
  138.2 11.7 %cholesky.44 = f32[128,128]{1,0:T(8,128)S(1)} custom-call(f32[128,128]{1,0:T(8,128)S(1)} %fusion.12), custom_call_target="Cholesky" | custom-call | tf_op jit(solution)/shard_map/jit(cholesky)/cholesky | solution.py:107
  150.0 0.6 compare_reduce_fusion.1
  150.6 0.7 fusion.2
  151.3 9.8 %custom-call.8 = f32[1,128,128]{1,2,0:T(8,128)S(1)} custom-call(f32[1,128,128]{2,1,0:T(8,128)S(1)} %fusion.2), custom_call_target="InvertDiagBlocksLowerTriangular" | custom-call | tf_op jit(solution)/shard_map/jit(_cho_solve)/triangular_solve | solution.py:108
  161.1 0.3 fusion.7
  161.4 0.2 fusion.9
  161.6 0.1 copy.56
  161.7 0.3 convolution_subtract_fusion
  162.0 0.1 copy.63
  162.1 11.7 %cholesky.55 = f32[128,128]{1,0:T(8,128)S(1)} custom-call(f32[128,128]{1,0:T(8,128)S(1)} %fusion.6), custom_call_target="Cholesky" | custom-call | tf_op jit(solution)/shard_map/jit(cholesky)/cholesky | solution.py:107
  173.8 0.6 compare_reduce_fusion
  174.5 0.7 fusion.3
  175.1 9.8 %custom-call.9 = f32[1,128,128]{1,2,0:T(8,128)S(1)} custom-call(f32[1,128,128]{2,1,0:T(8,128)S(1)} %fusion.3), custom_call_target="InvertDiagBlocksLowerTriangular" | custom-call | tf_op jit(solution)/shard_map/jit(_cho_solve)/triangular_solve | solution.py:108
  185.0 0.3 fusion
  185.3 0.8 convolution_bitcast_fusion
  186.1 0.7 copy.64
  (25 shorter events, 0.3 us)
Async XLA Ops:
  0.6 23.0 %copy-start = (bf16[192,2,4096]{2,1,0:T(2,128)(2,1)S(1)}, bf16[192,2,4096]{2,1,0:T(2,128)(2,1)}, u32[]{:S(2)}) copy-start(bf16[192,2,4096]{2,1,0:T(2,128)(2,1)} %param.5) | copy-start | bytes 9437188
  9.9 36.6 %all-to-all-start.2 = ((f32[64,1,2]{2,1,0:T(1,128)}), f32[64,1,2]{2,1,0:T(1,128)S(1)}, u32[]{:S(2)}, u32[]{:S(2)}) async-start(f32[64,1,2]{2,1,0:T(1,128)} %broadcast_in_dim.18), calls=%async_computation.2 | async-start | bytes 65536 | tf_op jit(solution)/shard_map/all_to_all | solution.py:132
  46.5 5.8 %copy-start.1 = (bf16[192,4096]{1,0:T(8,128)(2,1)S(1)}, bf16[192,4096]{1,0:T(8,128)(2,1)}, u32[]{:S(2)}) copy-start(bf16[192,4096]{1,0:T(8,128)(2,1)} %get-tuple-element.20) | copy-start | bytes 4718596
  46.5 25.9 %all-to-all-start = ((bf16[16,192,256]{2,1,0:T(8,128)(2,1)}), bf16[16,192,256]{2,1,0:T(8,128)(2,1)S(1)}, u32[]{:S(2)}, u32[]{:S(2)}) async-start(bf16[16,192,256]{2,1,0:T(8,128)(2,1)} %reshape.21), calls=%async_computation | async-start | bytes 3145728 | tf_op jit(solution)/shard_map/all_to_all | solution.py:127
  72.4 24.1 %all-to-all-start.1 = ((bf16[16,192,256]{2,1,0:T(8,128)(2,1)}), bf16[16,192,256]{2,1,0:T(8,128)(2,1)S(1)}, u32[]{:S(2)}, u32[]{:S(2)}) async-start(bf16[16,192,256]{2,1,0:T(8,128)(2,1)} %reshape.22), calls=%async_computation.1 | async-start | bytes 3145728 | tf_op jit(solution)/shard_map/all_to_all | solution.py:127
  77.2 23.9 %collective-permute-start = (bf16[16,192,256]{2,1,0:T(8,128)(2,1)S(1)}, bf16[16,192,256]{2,1,0:T(8,128)(2,1)}, u32[]{:S(2)}, u32[]{:S(2)}) collective-permute-start(bf16[16,192,256]{2,1,0:T(8,128)(2,1)S(1)} %all-to-all-done.x0_ref), channel_id=1, source_target_pairs={{64,0},{65,1},{66,2},{67,3},{68,4},{69,5},{70,6},{71,7},{72,8},{73... | collective-permute-start | bytes 4718600 | tf_op jit(solution)/shard_map/ppermute | solution.py:135
  96.5 21.9 %copy-start.2 = (f32[2]{0:T(128)S(1)}, f32[2]{0:T(128)}, u32[]{:S(2)}) copy-start(f32[2]{0:T(128)} %reduce_sum.19) | copy-start | bytes 28
  96.5 21.9 %copy-start.3 = (f32[2]{0:T(128)S(1)}, f32[2]{0:T(128)}, u32[]{:S(2)}) copy-start(f32[2]{0:T(128)} %param.6) | copy-start | bytes 28
  109.1 27.2 %collective-permute-start.4 = (f32[264,128]{1,0:T(8,128)}, f32[264,128]{1,0:T(8,128)S(1)}, u32[]{:S(2)}, u32[]{:S(2)}) collective-permute-start(f32[264,128]{1,0:T(8,128)} %get-tuple-element.11), channel_id=1, source_target_pairs={{0,36},{1,37},{2,4},{3,5},{4,32},{5,33},{6,0},{7,1},{8,44},{9,45},... | collective-permute-start | bytes 405512 | tf_op jit(solution)/shard_map/ppermute | solution.py:139
  116.2 20.1 %collective-permute-start.3 = (f32[264,128]{1,0:T(8,128)S(1)}, f32[264,128]{1,0:T(8,128)S(1)}, u32[]{:S(2)}, u32[]{:S(2)}) collective-permute-start(f32[264,128]{1,0:T(8,128)S(1)} %get-tuple-element.10), channel_id=1, source_target_pairs={{0,32},{1,33},{2,0},{3,1},{4,36},{5,37},{6,4},{7,5},{8,40},{9,41},... | collective-permute-start | bytes 405512 | tf_op jit(solution)/shard_map/ppermute | solution.py:139
  116.2 20.1 %collective-permute-start.1 = (f32[264,128]{1,0:T(8,128)S(1)}, f32[264,128]{1,0:T(8,128)S(1)}, u32[]{:S(2)}, u32[]{:S(2)}) collective-permute-start(f32[264,128]{1,0:T(8,128)S(1)} %get-tuple-element.8), channel_id=1, source_target_pairs={{0,0},{1,1},{2,32},{3,33},{4,4},{5,5},{6,36},{7,37},{8,8},{9,9},{1... | collective-permute-start | bytes 405512 | tf_op jit(solution)/shard_map/ppermute | solution.py:139
  116.9 19.5 %collective-permute-start.2 = (f32[264,128]{1,0:T(8,128)S(1)}, f32[264,128]{1,0:T(8,128)S(1)}, u32[]{:S(2)}, u32[]{:S(2)}) collective-permute-start(f32[264,128]{1,0:T(8,128)S(1)} %get-tuple-element.9), channel_id=1, source_target_pairs={{0,4},{1,5},{2,36},{3,37},{4,0},{5,1},{6,32},{7,33},{8,12},{9,13},... | collective-permute-start | bytes 405512 | tf_op jit(solution)/shard_map/ppermute | solution.py:139
  118.4 17.2 %collective-permute-start.5 = (f32[2]{0:T(128)S(1)}, f32[2]{0:T(128)S(1)}, u32[]{:S(2)}, u32[]{:S(2)}) collective-permute-start(f32[2]{0:T(128)S(1)} %multiply_multiply_fusion), channel_id=1, source_target_pairs={{64,0},{128,64},{192,128},{65,1},{129,65},{193,129},{66,2},{130,66... | collective-permute-start | bytes 32 | tf_op jit(solution)/shard_map/ppermute | solution.py:134

commit v2 on v1

v2 whole, which is shorter than its diff:
```python
from functools import partial

import jax
import jax.numpy as jnp
from jax import lax
from jax.experimental import pallas as pl
from jax.experimental.pallas import tpu as pltpu
from jax.sharding import PartitionSpec as P

B = 128
PANEL = 8
PARTS = 3
EVERY = ("section", "dp")


def dp_index(y1, y0, xl, z2, z1, z0):
    return ((((y1 * 2 + y0) * 2 + xl) * 2 + z2) * 2 + z1) * 2 + z0


def flipped(section):
    return section // 2


BITS = [tuple((d >> s) & 1 for s in (5, 4, 3, 2, 1, 0)) for d in range(64)]


def column_groups():
    groups = []
    for section in range(4):
        for z2 in range(2):
            for z1 in range(2):
                groups.append(
                    [
                        section * 64 + dp_index(m >> 3, (m >> 2) & 1, ((m >> 1) & 1) ^ flipped(section), z2, z1, m & 1)
                        for m in range(16)
                    ]
                )
    return groups


def following_route():
    route = []
    for section in range(1, 4):
        turn = flipped(section) ^ flipped(section - 1)
        for d, (y1, y0, xl, z2, z1, z0) in enumerate(BITS):
            route.append((section * 64 + d, (section - 1) * 64 + dp_index(y1, y0, xl ^ turn, z2, z1, z0)))
    return route


def home_route(a, b):
    route = []
    for section in range(4):
        turn = flipped(section)
        for d, (y1, y0, xl, z2, z1, z0) in enumerate(BITS):
            route.append((section * 64 + d, section * 64 + dp_index(z1 ^ a, y0, xl ^ turn, z2 ^ b, y1, z0)))
    return route


def member_block(m, zz):
    z1, y0, xl, z0 = m >> 3, (m >> 2) & 1, (m >> 1) & 1, m & 1
    return (((y0 * 2 + xl) * 2 + zz) * 2 + z1) * 2 + z0


def parts_of(value):
    parts = []
    for _ in range(PARTS):
        part = value.astype(jnp.bfloat16)
        parts.append(part)
        value = value - part.astype(jnp.float32)
    return parts


def columns_kernel(layer, damping_ref, x_ref, out_ref):
    groups = x_ref.shape[0]
    squares = jnp.zeros((PANEL, B), jnp.float32)
    for m in range(16):
        for zz in range(2):
            k = member_block(m, zz)
            cut = x_ref[:, layer, :, k * B : (k + 1) * B]
            out_ref[m, zz * groups : (zz + 1) * groups] = cut
            wide = cut.astype(jnp.float32)
            squares = squares + jnp.sum(wide * wide, axis=0)
    squares = jnp.broadcast_to(jnp.sum(squares, axis=0, keepdims=True), (PANEL, B))
    damping = jnp.full((PANEL, B), damping_ref[layer])
    row = lax.broadcasted_iota(jnp.int32, (PANEL, B), 0)
    extra = jnp.zeros((PANEL, B), jnp.float32)
    for i, part in enumerate(parts_of(squares) + parts_of(damping)):
        extra = jnp.where(row == i, part.astype(jnp.float32), extra)
    extra = extra.astype(jnp.bfloat16)
    for m in range(16):
        out_ref[m, 2 * groups] = extra


def sent_columns(x, damping, layer):
    groups = x.shape[0]
    vmem = pl.BlockSpec(memory_space=pltpu.VMEM)
    out = pl.pallas_call(
        partial(columns_kernel, layer),
        out_shape=jax.ShapeDtypeStruct((16, 2 * groups + 1, PANEL, B), jnp.bfloat16),
        in_specs=[pl.BlockSpec(memory_space=pltpu.SMEM), vmem],
        out_specs=vmem,
        name="sent_columns",
        cost_estimate=pl.CostEstimate(flops=2 * 2**20, bytes_accessed=2 * 2**21, transcendentals=0),
        compiler_params=pltpu.CompilerParams(vmem_limit_bytes=16 * 2**20),
    )(damping, x)
    return out.reshape(16, (2 * groups + 1) * PANEL, B)


def level_rows(x_ref):
    rows = x_ref.shape[1]
    total = jnp.zeros((PANEL, B), jnp.float32)
    for j in range(x_ref.shape[0]):
        total = total + x_ref[j, rows - PANEL :, :].astype(jnp.float32)
    last = x_ref[0, rows - PANEL :, :].astype(jnp.float32)
    squares = jnp.sum(total[:PARTS], axis=0, keepdims=True)
    damping = jnp.sum(last[PARTS : 2 * PARTS], axis=0, keepdims=True)
    return squares, damping * 0.25


def gram_kernel(pos_ref, x0_ref, x1_ref, x2_ref, *out_refs):
    turn, z2, z1 = pos_ref[0], pos_ref[1], pos_ref[2]
    chunks = x0_ref.shape[0]
    rows = (x0_ref.shape[1] - PANEL) // 2
    row = lax.broadcasted_iota(jnp.int32, (B, B), 0)
    col = lax.broadcasted_iota(jnp.int32, (B, B), 1)
    dims = (((0,), (0,)), ((), ()))

    def gram(left, *rights):
        right = jnp.concatenate(rights, axis=1) if len(rights) > 1 else rights[0]
        return lax.dot_general(left, right, dims, preferred_element_type=jnp.float32)

    levels = [level_rows(x_ref) for x_ref in (x0_ref, x1_ref, x2_ref)]
    for zz in range(2):
        cut = pl.ds(zz * rows, rows)
        first = jnp.zeros((B, 2 * B), jnp.float32)
        second = jnp.zeros((B, 2 * B), jnp.float32)
        third = jnp.zeros((B, B), jnp.float32)
        for j in range(chunks):
            x0 = x0_ref[j, cut, :]
            x1 = x1_ref[j, cut, :]
            x2 = x2_ref[j ^ (turn * 2), cut, :]
            first = first + gram(x0, x0, x1)
            second = second + gram(x1, x1, x2)
            third = third + gram(x2, x2)
        d0, d1, d2, c01, c12 = first[:, :B], second[:, :B], third, first[:, B:], second[:, B:]
        for layer, (d, n, c) in enumerate(((d0, d1, c01), (d1, d2, c12))):
            packed = jnp.where(row >= col, d, n)
            edge = jnp.sum(jnp.where(row == col, n, 0.0), axis=0, keepdims=True)
            for b in range(2):
                for a in range(2):

                    @pl.when(jnp.logical_and((z2 ^ b) == zz, (z1 ^ a) == layer))
                    def _():
                        out = out_refs[a * 2 + b]
                        out[0:B, :] = c
                        out[B : 2 * B, :] = packed
                        out[2 * B : 2 * B + 1, :] = edge
                        for i in range(2):
                            out[2 * B + 1 + i : 2 * B + 2 + i, :] = levels[layer + i][0]
                            out[2 * B + 3 + i : 2 * B + 4 + i, :] = levels[layer + i][1]
                        out[2 * B + 5 : 2 * B + 8, :] = jnp.zeros((3, B), jnp.float32)


def partial_grams(x0, x1, x2, position):
    vmem = pl.BlockSpec(memory_space=pltpu.VMEM)
    return pl.pallas_call(
        gram_kernel,
        out_shape=[jax.ShapeDtypeStruct((2 * B + PANEL, B), jnp.float32)] * 4,
        in_specs=[pl.BlockSpec(memory_space=pltpu.SMEM), vmem, vmem, vmem],
        out_specs=[vmem] * 4,
        name="partial_grams",
        cost_estimate=pl.CostEstimate(flops=10 * 3072 * B * B * 2, bytes_accessed=6 * 3072 * B * 2, transcendentals=0),
        compiler_params=pltpu.CompilerParams(vmem_limit_bytes=24 * 2**20),
    )(position, x0, x1, x2)


def inverted(panels):
    sub = lax.broadcasted_iota(jnp.int32, (PANEL, B), 0)
    lane = lax.broadcasted_iota(jnp.int32, (PANEL, B), 1)
    count = B // PANEL
    panels = list(panels)
    for k in range(count):
        first = k * PANEL
        here = jnp.logical_and(lane >= first, lane < first + PANEL)
        spread = [[jnp.broadcast_to(p[:, first + j : first + j + 1], (PANEL, B)) for j in range(PANEL)] for p in panels]
        own = spread[k]
        panel = jnp.where(here, jnp.where(lane - first == sub, 1.0, 0.0), panels[k])
        for j in range(PANEL):
            scale = 1.0 / own[j][j : j + 1, :]
            for q in range(j + 1, PANEL):
                top = own[q][j : j + 1, :] * scale
                own[q] = jnp.where(sub == j, top, own[q] - own[j] * top)
            top = panel[j : j + 1, :] * scale
            panel = jnp.where(sub == j, top, panel - own[j] * top)
        tops = [jnp.broadcast_to(panel[j : j + 1, :], (PANEL, B)) for j in range(PANEL)]
        for i in range(count):
            if i != k:
                rest = jnp.where(here, 0.0, panels[i])
                for j in range(PANEL):
                    rest = rest - spread[i][j] * tops[j]
                panels[i] = rest
        panels[k] = panel
    return panels


def cut_panels(square):
    return [square[i * PANEL : (i + 1) * PANEL, :] for i in range(B // PANEL)]


def solve_kernel(tokens, width, last_ref, *refs):
    arrived, (inverse_ref, coupling_ref) = refs[:4], refs[4:]
    owned = arrived[0][...] + arrived[1][...] + arrived[2][...] + arrived[3][...]
    row = lax.broadcasted_iota(jnp.int32, (B, B), 0)
    col = lax.broadcasted_iota(jnp.int32, (B, B), 1)
    edge = owned[2 * B :]
    mean = jnp.sum(edge, axis=1, keepdims=True) / tokens / width
    level, level_after = mean[1:2] * edge[3:4], mean[2:3] * edge[4:5]
    packed = owned[B : 2 * B] / tokens
    turned = packed.T
    damped = jnp.where(row >= col, packed, turned) + jnp.where(row == col, level, 0.0)
    diagonal = edge[0:1] / tokens + level_after
    following = jnp.where(row == col, diagonal, jnp.where(row < col, packed, turned))
    final = last_ref[0] == 1
    following = jnp.where(final, jnp.where(row == col, 1.0, 0.0), following)
    cross = jnp.where(final, 0.0, owned[:B] / tokens)
    solved = jnp.concatenate(inverted(cut_panels(following)), axis=0)
    coupling = jnp.dot(cross, solved, precision=lax.Precision.HIGHEST, preferred_element_type=jnp.float32)
    coupling_ref[0] = coupling
    product = lax.dot_general(
        coupling, cross, (((1,), (1,)), ((), ())), precision=lax.Precision.HIGHEST, preferred_element_type=jnp.float32
    )
    schur = damped - product
    schur = (schur + schur.T) * 0.5
    for i, panel in enumerate(inverted(cut_panels(schur))):
        inverse_ref[0, i * PANEL : (i + 1) * PANEL, :] = panel


def solved_blocks(arrived, last, tokens, width):
    vmem = pl.BlockSpec(memory_space=pltpu.VMEM)
    return pl.pallas_call(
        partial(solve_kernel, float(tokens), float(width)),
        out_shape=[jax.ShapeDtypeStruct((1, B, B), jnp.float32)] * 2,
        in_specs=[pl.BlockSpec(memory_space=pltpu.SMEM)] + [vmem] * 4,
        out_specs=[vmem] * 2,
        name="solved_blocks",
        cost_estimate=pl.CostEstimate(flops=10**7, bytes_accessed=6 * B * B * 8, transcendentals=0),
        compiler_params=pltpu.CompilerParams(vmem_limit_bytes=16 * 2**20),
    )(last, *arrived)


def local(activations, damping):
    token_rows, local_layers, model_width = activations.shape
    group_size = lax.axis_size("dp")
    section_count = lax.axis_size("section")
    section = lax.axis_index("section")
    dp = lax.axis_index("dp")
    groups = column_groups()
    by_layer = activations.reshape(token_rows // PANEL, PANEL, local_layers, model_width).transpose(0, 2, 1, 3)
    by_layer = lax.optimization_barrier(by_layer)

    def exchanged(columns):
        return lax.all_to_all(columns, EVERY, split_axis=0, concat_axis=0, axis_index_groups=groups, tiled=True)

    x0 = exchanged(sent_columns(by_layer, damping, 0))
    x2 = lax.ppermute(x0, EVERY, following_route())
    x1 = exchanged(sent_columns(by_layer, damping, 1))
    position = jnp.stack([section == 1, (dp >> 2) & 1, (dp >> 1) & 1]).astype(jnp.int32)
    sent = partial_grams(x0, x1, x2, position)
    arrived = [lax.ppermute(sent[a * 2 + b], EVERY, home_route(a, b)) for a in range(2) for b in range(2)]
    last = jnp.logical_and(section == section_count - 1, dp // (group_size // local_layers) == local_layers - 1)
    return tuple(solved_blocks(arrived, last.astype(jnp.int32)[None], token_rows * group_size, model_width))


def solution(mesh):
    placed = (P("dp", "section", None), P("section"))
    return jax.shard_map(
        local,
        mesh=mesh,
        in_specs=placed,
        out_specs=(P(("section", "dp"), None, None), P(("section", "dp"), None, None)),
        check_vma=False,
    )
```

time: 187 us -> 109 us (0.58)
  the two profiles are of different devices: /device:TPU:1 before, /device:TPU:228 now
where the time goes in v2:
time: 109 us
  waiting for transfers between devices  53.5 us (49%)
  starting transfers between devices  29.8 us (27%)
  Pallas kernels  18.1 us (17%)
  local copies, waits for them, and re-layouts  6.3 us (6%)
    all_to_all x2, waiting for transfers between devices, exchanged(): lax.all_to_all(columns, EVERY, split_axis=0, concat_axis=0, axis_index_gr...  37.8 us
    ppermute x4, waiting for transfers between devices, local(): lax.ppermute(sent[a * 2 + b], EVERY, home_route(a, b))  15 us
    ppermute x4, starting transfers between devices, local(): lax.ppermute(sent[a * 2 + b], EVERY, home_route(a, b))  14.7 us
    all_to_all x2, starting transfers between devices, exchanged(): lax.all_to_all(columns, EVERY, split_axis=0, concat_axis=0, axis_index_gr...  13.2 us
    pallas_call x1, Pallas kernels, solved_blocks(): pl.pallas_call(partial(solve_kernel, float(tokens), float(width)), out_sh...  10.2 us
    pallas_call x1, Pallas kernels, partial_grams(): pl.pallas_call(gram_kernel, out_shape=[jax.ShapeDtypeStruct((2 * B + PANE...  5.91 us
    reshape x1, local copies, waits for them, and re-layouts, local(): activations.reshape(token_rows // PANEL, PANEL, local_layers, model_width)  3.97 us
    unnamed x6, local copies, waits for them, and re-layouts  2.32 us
  transfers between devices with their start and end apart: 7, of which 5 were waited for; matrix products, arithmetic and copies ran while one was open for 0% of the time, Pallas kernels for 1%

profile of v2, /device:TPU:228, one launch (start us, length us, event | category | flops | bytes accessed | tf_op | source)
XLA Modules:
  0.0 108.5 jit_solution(2113779502358462061)
XLA Ops:
  0.6 0.0 copy-start.2
  0.6 4.0 %copy.9 = bf16[24,8,2,4096]{3,1,2,0:T(8,128)(2,1)S(1)} copy(bf16[24,8,2,4096]{3,2,1,0:T(2,128)(2,1)} %bitcast.14) | data formatting | bytes 6291456 | tf_op jit(solution)/shard_map/reshape | solution.py:258
  4.6 0.0 copy-done.2
  4.6 1.0 sent_columns.2
  5.6 0.0 copy-start.1
  5.7 1.2 %copy-done.1 = bf16[16,49,8,128]{3,2,1,0:T(8,128)(2,1)} copy-done((bf16[16,49,8,128]{3,2,1,0:T(8,128)(2,1)}, bf16[16,49,8,128]{3,2,1,0:T(8,128)(2,1)S(1)}, u32[]{:S(2)}) %copy-start.1) | copy-done | bytes 1605656
  6.8 6.8 %all-to-all-start = ((bf16[16,392,128]{2,1,0:T(8,128)(2,1)}), bf16[16,392,128]{2,1,0:T(8,128)(2,1)}, u32[]{:S(2)}, u32[]{:S(2)}) async-start(bf16[16,392,128]{2,1,0:T(8,128)(2,1)} %bitcast.13), calls=%async_computation | async-start | bytes 3211264 | tf_op jit(solution)/shard_map/all_to_all | solution.py:262
  13.7 1.0 sent_columns.3
  14.7 0.0 copy-start
  14.7 1.1 %copy-done = bf16[16,49,8,128]{3,2,1,0:T(8,128)(2,1)} copy-done((bf16[16,49,8,128]{3,2,1,0:T(8,128)(2,1)}, bf16[16,49,8,128]{3,2,1,0:T(8,128)(2,1)S(1)}, u32[]{:S(2)}) %copy-start) | copy-done | bytes 1605656
  15.8 20.0 %all-to-all-done.x0_ref = bf16[16,392,128]{2,1,0:T(8,128)(2,1)} async-done(((bf16[16,392,128]{2,1,0:T(8,128)(2,1)}), bf16[16,392,128]{2,1,0:T(8,128)(2,1)}, u32[]{:S(2)}, u32[]{:S(2)}) %all-to-all-start) | async-done | bytes 1605664 | tf_op jit(solution)/shard_map/all_to_all | solution.py:262
  35.9 6.3 %all-to-all-start.1 = ((bf16[16,392,128]{2,1,0:T(8,128)(2,1)}), bf16[16,392,128]{2,1,0:T(8,128)(2,1)S(1)}, u32[]{:S(2)}, u32[]{:S(2)}) async-start(bf16[16,392,128]{2,1,0:T(8,128)(2,1)} %bitcast.12), calls=%async_computation.1 | async-start | bytes 3211264 | tf_op jit(solution)/shard_map/all_to_all | solution.py:262
  42.2 1.9 %collective-permute-start = (bf16[16,392,128]{2,1,0:T(8,128)(2,1)}, bf16[16,392,128]{2,1,0:T(8,128)(2,1)S(1)}, u32[]{:S(2)}, u32[]{:S(2)}) collective-permute-start(bf16[16,392,128]{2,1,0:T(8,128)(2,1)} %all-to-all-done.x0_ref), channel_id=1, source_target_pairs={{64,0},{65,1},{66,2},{67,3},{68,4},{69,5},{70,6},{71,7},{72,8},{73... | collective-permute-start | bytes 4816904 | tf_op jit(solution)/shard_map/ppermute | solution.py:265
  44.2 0.1 pad_add_fusion.pos_ref
  44.2 17.8 %all-to-all-done.1.x1_ref = bf16[16,392,128]{2,1,0:T(8,128)(2,1)S(1)} async-done(((bf16[16,392,128]{2,1,0:T(8,128)(2,1)}), bf16[16,392,128]{2,1,0:T(8,128)(2,1)S(1)}, u32[]{:S(2)}, u32[]{:S(2)}) %all-to-all-start.1) | async-done | bytes 1605664 | tf_op jit(solution)/shard_map/all_to_all | solution.py:262
  62.0 0.7 collective-permute-done.x2_ref
  62.7 5.9 %partial_grams.1 = (f32[264,128]{1,0:T(8,128)}, f32[264,128]{1,0:T(8,128)}, f32[264,128]{1,0:T(8,128)S(1)}, f32[264,128]{1,0:T(8,128)S(1)}) custom-call(s32[3]{0:T(128)S(1)} %pad_add_fusion.pos_ref, bf16[16,392,128]{2,1,0:T(8,128)(2,1)} %all-to-all-done.x0_ref, bf16[16,392,128]{2,1,0:T(8,128)(2,1)S(1)} %all-to-all-done.1.x1_ref, ...), custom_call_target="tpu_custom_call" | custom-call | flops 1006632960 | bytes 4718592 | tf_op jit(solution)/shard_map/partial_grams/pallas_call | solution.py:166
  68.6 5.8 %collective-permute-start.1 = (f32[264,128]{1,0:T(8,128)}, f32[264,128]{1,0:T(8,128)S(1)}, u32[]{:S(2)}, u32[]{:S(2)}) collective-permute-start(f32[264,128]{1,0:T(8,128)} %get-tuple-element.6), channel_id=1, source_target_pairs={{0,0},{1,1},{2,32},{3,33},{4,4},{5,5},{6,36},{7,37},{8,8},{9,9},{1... | collective-permute-start | bytes 405512 | tf_op jit(solution)/shard_map/ppermute | solution.py:269
  74.4 1.5 %collective-permute-start.2 = (f32[264,128]{1,0:T(8,128)}, f32[264,128]{1,0:T(8,128)S(1)}, u32[]{:S(2)}, u32[]{:S(2)}) collective-permute-start(f32[264,128]{1,0:T(8,128)} %get-tuple-element.7), channel_id=1, source_target_pairs={{0,4},{1,5},{2,36},{3,37},{4,0},{5,1},{6,32},{7,33},{8,12},{9,13},... | collective-permute-start | bytes 405512 | tf_op jit(solution)/shard_map/ppermute | solution.py:269
  75.9 0.0 collective-permute-start.3
  75.9 7.4 %collective-permute-start.4 = (f32[264,128]{1,0:T(8,128)S(1)}, f32[264,128]{1,0:T(8,128)S(1)}, u32[]{:S(2)}, u32[]{:S(2)}) collective-permute-start(f32[264,128]{1,0:T(8,128)S(1)} %get-tuple-element.9), channel_id=1, source_target_pairs={{0,36},{1,37},{2,4},{3,5},{4,32},{5,33},{6,0},{7,1},{8,44},{9,45},... | collective-permute-start | bytes 405512 | tf_op jit(solution)/shard_map/ppermute | solution.py:269
  83.4 9.4 %collective-permute-done.1.refs_0_ = f32[264,128]{1,0:T(8,128)S(1)} collective-permute-done((f32[264,128]{1,0:T(8,128)}, f32[264,128]{1,0:T(8,128)S(1)}, u32[]{:S(2)}, u32[]{:S(2)}) %collective-permute-start.1) | collective-permute-done | bytes 135200 | tf_op jit(solution)/shard_map/ppermute | solution.py:269
  92.7 0.0 collective-permute-done.2.refs_1_
  92.7 5.6 %collective-permute-done.3.refs_2_ = f32[264,128]{1,0:T(8,128)S(1)} collective-permute-done((f32[264,128]{1,0:T(8,128)S(1)}, f32[264,128]{1,0:T(8,128)S(1)}, u32[]{:S(2)}, u32[]{:S(2)}) %collective-permute-start.3) | collective-permute-done | bytes 135200 | tf_op jit(solution)/shard_map/ppermute | solution.py:269
  98.3 0.0 collective-permute-done.4.refs_3_
  98.3 10.2 %solved_blocks.1 = (f32[1,128,128]{2,1,0:T(8,128)}, f32[1,128,128]{2,1,0:T(8,128)}) custom-call(s32[1]{0:T(128)} %bitcast.last_ref, f32[264,128]{1,0:T(8,128)S(1)} %collective-permute-done.1.refs_0_, f32[264,128]{1,0:T(8,128)S(1)} %collective-permute-done.2.refs_1_, f32[264,128]{1,0:T(8,128)S(1)} %collective-permute-done.3.refs_2_, ...), custom_call_target="tpu_custom_call" | custom-call | flops 10000000 | bytes 786432 | tf_op jit(solution)/shard_map/solved_blocks/pallas_call | solution.py:240
Async XLA Ops:
  0.6 4.0 %copy-start.2 = (f32[2]{0:T(128)S(1)}, f32[2]{0:T(128)}, u32[]{:S(2)}) copy-start(f32[2]{0:T(128)} %damping_ref.3) | copy-start | bytes 28
  5.6 1.2 %copy-start.1 = (bf16[16,49,8,128]{3,2,1,0:T(8,128)(2,1)}, bf16[16,49,8,128]{3,2,1,0:T(8,128)(2,1)S(1)}, u32[]{:S(2)}) copy-start(bf16[16,49,8,128]{3,2,1,0:T(8,128)(2,1)S(1)} %sent_columns.2) | copy-start | bytes 4816900
  6.8 29.1 %all-to-all-start = ((bf16[16,392,128]{2,1,0:T(8,128)(2,1)}), bf16[16,392,128]{2,1,0:T(8,128)(2,1)}, u32[]{:S(2)}, u32[]{:S(2)}) async-start(bf16[16,392,128]{2,1,0:T(8,128)(2,1)} %bitcast.13), calls=%async_computation | async-start | bytes 3211264 | tf_op jit(solution)/shard_map/all_to_all | solution.py:262
  14.7 1.2 %copy-start = (bf16[16,49,8,128]{3,2,1,0:T(8,128)(2,1)}, bf16[16,49,8,128]{3,2,1,0:T(8,128)(2,1)S(1)}, u32[]{:S(2)}) copy-start(bf16[16,49,8,128]{3,2,1,0:T(8,128)(2,1)S(1)} %sent_columns.3) | copy-start | bytes 4816900
  35.9 26.1 %all-to-all-start.1 = ((bf16[16,392,128]{2,1,0:T(8,128)(2,1)}), bf16[16,392,128]{2,1,0:T(8,128)(2,1)S(1)}, u32[]{:S(2)}, u32[]{:S(2)}) async-start(bf16[16,392,128]{2,1,0:T(8,128)(2,1)} %bitcast.12), calls=%async_computation.1 | async-start | bytes 3211264 | tf_op jit(solution)/shard_map/all_to_all | solution.py:262
  42.2 20.5 %collective-permute-start = (bf16[16,392,128]{2,1,0:T(8,128)(2,1)}, bf16[16,392,128]{2,1,0:T(8,128)(2,1)S(1)}, u32[]{:S(2)}, u32[]{:S(2)}) collective-permute-start(bf16[16,392,128]{2,1,0:T(8,128)(2,1)} %all-to-all-done.x0_ref), channel_id=1, source_target_pairs={{64,0},{65,1},{66,2},{67,3},{68,4},{69,5},{70,6},{71,7},{72,8},{73... | collective-permute-start | bytes 4816904 | tf_op jit(solution)/shard_map/ppermute | solution.py:265
  68.6 24.1 %collective-permute-start.1 = (f32[264,128]{1,0:T(8,128)}, f32[264,128]{1,0:T(8,128)S(1)}, u32[]{:S(2)}, u32[]{:S(2)}) collective-permute-start(f32[264,128]{1,0:T(8,128)} %get-tuple-element.6), channel_id=1, source_target_pairs={{0,0},{1,1},{2,32},{3,33},{4,4},{5,5},{6,36},{7,37},{8,8},{9,9},{1... | collective-permute-start | bytes 405512 | tf_op jit(solution)/shard_map/ppermute | solution.py:269
  74.4 18.4 %collective-permute-start.2 = (f32[264,128]{1,0:T(8,128)}, f32[264,128]{1,0:T(8,128)S(1)}, u32[]{:S(2)}, u32[]{:S(2)}) collective-permute-start(f32[264,128]{1,0:T(8,128)} %get-tuple-element.7), channel_id=1, source_target_pairs={{0,4},{1,5},{2,36},{3,37},{4,0},{5,1},{6,32},{7,33},{8,12},{9,13},... | collective-permute-start | bytes 405512 | tf_op jit(solution)/shard_map/ppermute | solution.py:269
  75.9 22.4 %collective-permute-start.3 = (f32[264,128]{1,0:T(8,128)S(1)}, f32[264,128]{1,0:T(8,128)S(1)}, u32[]{:S(2)}, u32[]{:S(2)}) collective-permute-start(f32[264,128]{1,0:T(8,128)S(1)} %get-tuple-element.8), channel_id=1, source_target_pairs={{0,32},{1,33},{2,0},{3,1},{4,36},{5,37},{6,4},{7,5},{8,40},{9,41},... | collective-permute-start | bytes 405512 | tf_op jit(solution)/shard_map/ppermute | solution.py:269
  75.9 22.4 %collective-permute-start.4 = (f32[264,128]{1,0:T(8,128)S(1)}, f32[264,128]{1,0:T(8,128)S(1)}, u32[]{:S(2)}, u32[]{:S(2)}) collective-permute-start(f32[264,128]{1,0:T(8,128)S(1)} %get-tuple-element.9), channel_id=1, source_target_pairs={{0,36},{1,37},{2,4},{3,5},{4,32},{5,33},{6,0},{7,1},{8,44},{9,45},... | collective-permute-start | bytes 405512 | tf_op jit(solution)/shard_map/ppermute | solution.py:269

commit v3 on v2

--- a/solution.py
+++ b/solution.py
@@ -9,6 +9,7 @@
 
 B = 128
 PANEL = 8
+STEP = 16
 PARTS = 3
 EVERY = ("section", "dp")
 
@@ -117,32 +118,54 @@
     return squares, damping * 0.25
 
 
-def gram_kernel(pos_ref, x0_ref, x1_ref, x2_ref, *out_refs):
+def tokens_of(x_ref, zz, turn=0):
+    rows = (x_ref.shape[1] - PANEL) // 2
+    return jnp.concatenate([x_ref[j ^ (turn * 2), zz * rows : (zz + 1) * rows, :] for j in range(x_ref.shape[0])], axis=0)
+
+
+def gram(left, right):
+    return lax.dot_general(left, right, (((0,), (0,)), ((), ())), preferred_element_type=jnp.float32)
+
+
+def own_kernel(x_ref, gram_ref, level_ref, kept_ref):
+    squares, damping = level_rows(x_ref)
+    level_ref[0:1, :] = squares
+    level_ref[1:2, :] = damping
+    level_ref[2:PANEL, :] = jnp.zeros((PANEL - 2, B), jnp.float32)
+    for zz in range(2):
+        x = tokens_of(x_ref, zz)
+        kept_ref[zz] = x
+        gram_ref[zz] = gram(x, x)
+
+
+def own_grams(x):
+    vmem = pl.BlockSpec(memory_space=pltpu.VMEM)
+    return pl.pallas_call(
+        own_kernel,
+        out_shape=[
+            jax.ShapeDtypeStruct((2, B, B), jnp.float32),
+            jax.ShapeDtypeStruct((PANEL, B), jnp.float32),
+            jax.ShapeDtypeStruct((2, x.shape[0] * (x.shape[1] - PANEL) // 2, B), jnp.bfloat16),
+        ],
+        in_specs=[vmem],
+        out_specs=[vmem] * 3,
+        name="own_grams",
+        cost_estimate=pl.CostEstimate(flops=4 * 3072 * B * B, bytes_accessed=2 * 3072 * B * 2, transcendentals=0),
+        compiler_params=pltpu.CompilerParams(vmem_limit_bytes=16 * 2**20),
+    )(x)
+
+
+def gram_kernel(pos_ref, d0_ref, level_ref, x0_ref, x1_ref, x2_ref, *out_refs):
     turn, z2, z1 = pos_ref[0], pos_ref[1], pos_ref[2]
-    chunks = x0_ref.shape[0]
-    rows = (x0_ref.shape[1] - PANEL) // 2
     row = lax.broadcasted_iota(jnp.int32, (B, B), 0)
     col = lax.broadcasted_iota(jnp.int32, (B, B), 1)
-    dims = (((0,), (0,)), ((), ()))
-
-    def gram(left, *rights):
-        right = jnp.concatenate(rights, axis=1) if len(rights) > 1 else rights[0]
-        return lax.dot_general(left, right, dims, preferred_element_type=jnp.float32)
-
-    levels = [level_rows(x_ref) for x_ref in (x0_ref, x1_ref, x2_ref)]
+    levels = [(level_ref[0:1, :], level_ref[1:2, :])] + [level_rows(x_ref) for x_ref in (x1_ref, x2_ref)]
     for zz in range(2):
-        cut = pl.ds(zz * rows, rows)
-        first = jnp.zeros((B, 2 * B), jnp.float32)
-        second = jnp.zeros((B, 2 * B), jnp.float32)
-        third = jnp.zeros((B, B), jnp.float32)
-        for j in range(chunks):
-            x0 = x0_ref[j, cut, :]
-            x1 = x1_ref[j, cut, :]
-            x2 = x2_ref[j ^ (turn * 2), cut, :]
-            first = first + gram(x0, x0, x1)
-            second = second + gram(x1, x1, x2)
-            third = third + gram(x2, x2)
-        d0, d1, d2, c01, c12 = first[:, :B], second[:, :B], third, first[:, B:], second[:, B:]
+        x0, x1, x2 = x0_ref[zz], tokens_of(x1_ref, zz), tokens_of(x2_ref, zz, turn)
+        middle = gram(x1, jnp.concatenate([x1, x2], axis=1))
+        d0, d1, c12 = d0_ref[zz], middle[:, :B], middle[:, B:]
+        c01 = gram(x1, x0).T
+        d2 = gram(x2, x2)
         for layer, (d, n, c) in enumerate(((d0, d1, c01), (d1, d2, c12))):
             packed = jnp.where(row >= col, d, n)
             edge = jnp.sum(jnp.where(row == col, n, 0.0), axis=0, keepdims=True)
@@ -161,50 +184,60 @@
                         out[2 * B + 5 : 2 * B + 8, :] = jnp.zeros((3, B), jnp.float32)
 
 
-def partial_grams(x0, x1, x2, position):
+def partial_grams(d0, level0, x0, x1, x2, position):
     vmem = pl.BlockSpec(memory_space=pltpu.VMEM)
     return pl.pallas_call(
         gram_kernel,
         out_shape=[jax.ShapeDtypeStruct((2 * B + PANEL, B), jnp.float32)] * 4,
-        in_specs=[pl.BlockSpec(memory_space=pltpu.SMEM), vmem, vmem, vmem],
+        in_specs=[pl.BlockSpec(memory_space=pltpu.SMEM)] + [vmem] * 5,
         out_specs=[vmem] * 4,
         name="partial_grams",
-        cost_estimate=pl.CostEstimate(flops=10 * 3072 * B * B * 2, bytes_accessed=6 * 3072 * B * 2, transcendentals=0),
+        cost_estimate=pl.CostEstimate(flops=8 * 3072 * B * B * 2, bytes_accessed=6 * 3072 * B * 2, transcendentals=0),
         compiler_params=pltpu.CompilerParams(vmem_limit_bytes=24 * 2**20),
-    )(position, x0, x1, x2)
+    )(position, d0, level0, x0, x1, x2)
 
 
 def inverted(panels):
-    sub = lax.broadcasted_iota(jnp.int32, (PANEL, B), 0)
-    lane = lax.broadcasted_iota(jnp.int32, (PANEL, B), 1)
-    count = B // PANEL
+    sub = lax.broadcasted_iota(jnp.int32, (STEP, B), 0)
+    lane = lax.broadcasted_iota(jnp.int32, (STEP, B), 1)
+    count = B // STEP
     panels = list(panels)
+    nothing = jnp.zeros((STEP, B), jnp.float32)
+
+    def spread(panel, first):
+        return [jnp.broadcast_to(panel[:, first + j : first + j + 1], (STEP, B)) for j in range(STEP)]
+
     for k in range(count):
-        first = k * PANEL
-        here = jnp.logical_and(lane >= first, lane < first + PANEL)
-        spread = [[jnp.broadcast_to(p[:, first + j : first + j + 1], (PANEL, B)) for j in range(PANEL)] for p in panels]
-        own = spread[k]
+        first = k * STEP
+        here = jnp.logical_and(lane >= first, lane < first + STEP)
+        own = spread(panels[k], first)
         panel = jnp.where(here, jnp.where(lane - first == sub, 1.0, 0.0), panels[k])
-        for j in range(PANEL):
+        for j in range(STEP):
             scale = 1.0 / own[j][j : j + 1, :]
-            for q in range(j + 1, PANEL):
+            for q in range(j + 1, STEP):
                 top = own[q][j : j + 1, :] * scale
                 own[q] = jnp.where(sub == j, top, own[q] - own[j] * top)
             top = panel[j : j + 1, :] * scale
             panel = jnp.where(sub == j, top, panel - own[j] * top)
-        tops = [jnp.broadcast_to(panel[j : j + 1, :], (PANEL, B)) for j in range(PANEL)]
-        for i in range(count):
-            if i != k:
-                rest = jnp.where(here, 0.0, panels[i])
-                for j in range(PANEL):
-                    rest = rest - spread[i][j] * tops[j]
-                panels[i] = rest
+        following = k + 1 if k + 1 < count else None
+        rows = [i for i in range(count) if i != k and i != following]
+        left = jnp.concatenate([jnp.where(here, panels[i], 0.0) for i in rows], axis=0)
+        right = jnp.concatenate([panel if i == k else nothing for i in range(count)], axis=0)
+        product = jnp.dot(left, right, precision=lax.Precision.HIGHEST, preferred_element_type=jnp.float32)
+        for at, i in enumerate(rows):
+            panels[i] = jnp.where(here, 0.0, panels[i]) - product[at * STEP : (at + 1) * STEP]
+        if following is not None:
+            coefs = spread(panels[following], first)
+            rest = jnp.where(here, 0.0, panels[following])
+            for j in range(STEP):
+                rest = rest - coefs[j] * panel[j : j + 1, :]
+            panels[following] = rest
         panels[k] = panel
     return panels
 
 
 def cut_panels(square):
-    return [square[i * PANEL : (i + 1) * PANEL, :] for i in range(B // PANEL)]
+    return [square[i * STEP : (i + 1) * STEP, :] for i in range(B // STEP)]
 
 
 def solve_kernel(tokens, width, last_ref, *refs):
@@ -232,7 +265,7 @@
     schur = damped - product
     schur = (schur + schur.T) * 0.5
     for i, panel in enumerate(inverted(cut_panels(schur))):
-        inverse_ref[0, i * PANEL : (i + 1) * PANEL, :] = panel
+        inverse_ref[0, i * STEP : (i + 1) * STEP, :] = panel
 
 
 def solved_blocks(arrived, last, tokens, width):
@@ -265,7 +298,8 @@
     x2 = lax.ppermute(x0, EVERY, following_route())
     x1 = exchanged(sent_columns(by_layer, damping, 1))
     position = jnp.stack([section == 1, (dp >> 2) & 1, (dp >> 1) & 1]).astype(jnp.int32)
-    sent = partial_grams(x0, x1, x2, position)
+    d0, level0, kept = own_grams(x0)
+    sent = partial_grams(d0, level0, kept, x1, x2, position)
     arrived = [lax.ppermute(sent[a * 2 + b], EVERY, home_route(a, b)) for a in range(2) for b in range(2)]
     last = jnp.logical_and(section == section_count - 1, dp // (group_size // local_layers) == local_layers - 1)
     return tuple(solved_blocks(arrived, last.astype(jnp.int32)[None], token_rows * group_size, model_width))

time: 109 us -> 104 us (0.954)
  Pallas kernels: 18.1 us -> 13.9 us
  waiting for transfers between devices: 53.5 us -> 50.3 us
  local copies, waits for them, and re-layouts: 6.3 us -> 8.84 us
    pallas_call x1, Pallas kernels: 10.2 us -> 6.72 us  [solved_blocks(): pl.pallas_call(partial(solve_kernel, float(tokens), float(width)), out_sh...]
    all_to_all x2, waiting for transfers between devices: 37.8 us -> 34.6 us  [exchanged(): lax.all_to_all(columns, EVERY, split_axis=0, concat_axis=0, axis_index_gr...]
    pallas_call x1, Pallas kernels: 5.91 us -> 3.12 us  [partial_grams(): pl.pallas_call(gram_kernel, out_shape=[jax.ShapeDtypeStruct((2 * B + PANE...]
    unnamed x6 -> x10, local copies, waits for them, and re-layouts: 2.32 us -> 4.87 us
    pallas_call x0 -> x1, Pallas kernels: none -> 2.06 us  [own_grams(): pl.pallas_call(own_kernel, out_shape=[jax.ShapeDtypeStruct((2, B, B), jnp...]
  transfers between devices with their start and end apart: 7 -> 7, of which waited for: 5 -> 5; matrix products, arithmetic and copies ran while one was open for 0% -> 0% of each run, Pallas kernels for 1% -> 3%
where the time goes in v3:
time: 104 us
  waiting for transfers between devices  50.3 us (48%)
  starting transfers between devices  29.8 us (29%)
  Pallas kernels  13.9 us (13%)
  local copies, waits for them, and re-layouts  8.84 us (8%)
    all_to_all x2, waiting for transfers between devices, exchanged(): lax.all_to_all(columns, EVERY, split_axis=0, concat_axis=0, axis_index_gr...  34.6 us
    ppermute x4, waiting for transfers between devices, local(): lax.ppermute(sent[a * 2 + b], EVERY, home_route(a, b))  14.9 us
    ppermute x4, starting transfers between devices, local(): lax.ppermute(sent[a * 2 + b], EVERY, home_route(a, b))  14.7 us
    all_to_all x2, starting transfers between devices, exchanged(): lax.all_to_all(columns, EVERY, split_axis=0, concat_axis=0, axis_index_gr...  13.2 us
    pallas_call x1, Pallas kernels, solved_blocks(): pl.pallas_call(partial(solve_kernel, float(tokens), float(width)), out_sh...  6.72 us
    unnamed x10, local copies, waits for them, and re-layouts  4.87 us
    reshape x1, local copies, waits for them, and re-layouts, local(): activations.reshape(token_rows // PANEL, PANEL, local_layers, model_width)  3.97 us
    pallas_call x1, Pallas kernels, partial_grams(): pl.pallas_call(gram_kernel, out_shape=[jax.ShapeDtypeStruct((2 * B + PANE...  3.12 us
  transfers between devices with their start and end apart: 7, of which 5 were waited for; matrix products, arithmetic and copies ran while one was open for 0% of the time, Pallas kernels for 3%

profile of v3, /device:TPU:228, one launch (start us, length us, event | category | flops | bytes accessed | tf_op | source)
XLA Modules:
  0.0 103.7 jit_solution(533763401049323392)
XLA Ops:
  0.6 0.0 copy-start.4
  0.6 4.0 %copy.9 = bf16[24,8,2,4096]{3,1,2,0:T(8,128)(2,1)S(1)} copy(bf16[24,8,2,4096]{3,2,1,0:T(2,128)(2,1)} %bitcast.14) | data formatting | bytes 6291456 | tf_op jit(solution)/shard_map/reshape | solution.py:291
  4.6 0.0 copy-done.4
  4.6 1.0 sent_columns.2
  5.6 0.0 copy-start.1
  5.7 1.2 %copy-done.1 = bf16[16,49,8,128]{3,2,1,0:T(8,128)(2,1)} copy-done((bf16[16,49,8,128]{3,2,1,0:T(8,128)(2,1)}, bf16[16,49,8,128]{3,2,1,0:T(8,128)(2,1)S(1)}, u32[]{:S(2)}) %copy-start.1) | copy-done | bytes 1605656
  6.8 6.8 %all-to-all-start = ((bf16[16,392,128]{2,1,0:T(8,128)(2,1)}), bf16[16,392,128]{2,1,0:T(8,128)(2,1)}, u32[]{:S(2)}, u32[]{:S(2)}) async-start(bf16[16,392,128]{2,1,0:T(8,128)(2,1)} %bitcast.13), calls=%async_computation | async-start | bytes 3211264 | tf_op jit(solution)/shard_map/all_to_all | solution.py:295
  13.7 1.0 sent_columns.3
  14.7 0.0 copy-start
  14.7 1.1 %copy-done = bf16[16,49,8,128]{3,2,1,0:T(8,128)(2,1)} copy-done((bf16[16,49,8,128]{3,2,1,0:T(8,128)(2,1)}, bf16[16,49,8,128]{3,2,1,0:T(8,128)(2,1)S(1)}, u32[]{:S(2)}) %copy-start) | copy-done | bytes 1605656
  15.8 20.1 %all-to-all-done.x_ref = bf16[16,392,128]{2,1,0:T(8,128)(2,1)} async-done(((bf16[16,392,128]{2,1,0:T(8,128)(2,1)}), bf16[16,392,128]{2,1,0:T(8,128)(2,1)}, u32[]{:S(2)}, u32[]{:S(2)}) %all-to-all-start) | async-done | bytes 1605664 | tf_op jit(solution)/shard_map/all_to_all | solution.py:295
  35.9 6.3 %all-to-all-start.1 = ((bf16[16,392,128]{2,1,0:T(8,128)(2,1)}), bf16[16,392,128]{2,1,0:T(8,128)(2,1)S(1)}, u32[]{:S(2)}, u32[]{:S(2)}) async-start(bf16[16,392,128]{2,1,0:T(8,128)(2,1)} %bitcast.12), calls=%async_computation.1 | async-start | bytes 3211264 | tf_op jit(solution)/shard_map/all_to_all | solution.py:295
  42.2 1.9 %collective-permute-start = (bf16[16,392,128]{2,1,0:T(8,128)(2,1)}, bf16[16,392,128]{2,1,0:T(8,128)(2,1)S(1)}, u32[]{:S(2)}, u32[]{:S(2)}) collective-permute-start(bf16[16,392,128]{2,1,0:T(8,128)(2,1)} %all-to-all-done.x_ref), channel_id=1, source_target_pairs={{64,0},{65,1},{66,2},{67,3},{68,4},{69,5},{70,6},{71,7},{72,8},{73... | collective-permute-start | bytes 4816904 | tf_op jit(solution)/shard_map/ppermute | solution.py:298
  44.2 0.1 pad_add_fusion.pos_ref
  44.2 2.1 %own_grams.1 = (f32[2,128,128]{2,1,0:T(8,128)S(1)}, f32[8,128]{1,0:T(8,128)S(1)}, bf16[2,3072,128]{2,1,0:T(8,128)(2,1)S(1)}) custom-call(bf16[16,392,128]{2,1,0:T(8,128)(2,1)} %all-to-all-done.x_ref), custom_call_target="tpu_custom_call" | custom-call | flops 201326592 | bytes 1572864 | tf_op jit(solution)/shard_map/own_grams/pallas_call | solution.py:143
  46.3 0.0 copy-start.2
  46.3 1.1 %copy-done.2 = bf16[2,3072,128]{2,1,0:T(8,128)(2,1)} copy-done((bf16[2,3072,128]{2,1,0:T(8,128)(2,1)}, bf16[2,3072,128]{2,1,0:T(8,128)(2,1)S(1)}, u32[]{:S(2)}) %copy-start.2) | copy-done | bytes 1572888
  47.5 14.5 %all-to-all-done.1.x1_ref = bf16[16,392,128]{2,1,0:T(8,128)(2,1)S(1)} async-done(((bf16[16,392,128]{2,1,0:T(8,128)(2,1)}), bf16[16,392,128]{2,1,0:T(8,128)(2,1)S(1)}, u32[]{:S(2)}, u32[]{:S(2)}) %all-to-all-start.1) | async-done | bytes 1605664 | tf_op jit(solution)/shard_map/all_to_all | solution.py:295
  62.0 0.7 collective-permute-done.x2_ref
  62.7 0.0 copy-start.3
  62.7 1.4 %copy-done.3 = bf16[2,3072,128]{2,1,0:T(8,128)(2,1)S(1)} copy-done((bf16[2,3072,128]{2,1,0:T(8,128)(2,1)S(1)}, bf16[2,3072,128]{2,1,0:T(8,128)(2,1)}, u32[]{:S(2)}) %copy-start.3) | copy-done | bytes 1572888
  64.1 3.1 %partial_grams.1 = (f32[264,128]{1,0:T(8,128)}, f32[264,128]{1,0:T(8,128)}, f32[264,128]{1,0:T(8,128)}, f32[264,128]{1,0:T(8,128)S(1)}) custom-call(s32[3]{0:T(128)S(1)} %pad_add_fusion.pos_ref, f32[2,128,128]{2,1,0:T(8,128)S(1)} %get-tuple-element.9.d0_ref, f32[8,128]{1,0:T(8,128)S(1)} %get-tuple-element.10.level_ref, bf16[2,3072,128]{2,1,0:T(8,128)(2,1)S(1)} %copy-done.3, ...), custom_call_target="tpu_custom_call" | custom-call | flops 805306368 | bytes 4718592 | tf_op jit(solution)/shard_map/partial_grams/pallas_call | solution.py:189
  67.3 5.8 %collective-permute-start.1 = (f32[264,128]{1,0:T(8,128)}, f32[264,128]{1,0:T(8,128)S(1)}, u32[]{:S(2)}, u32[]{:S(2)}) collective-permute-start(f32[264,128]{1,0:T(8,128)} %get-tuple-element.12), channel_id=1, source_target_pairs={{0,0},{1,1},{2,32},{3,33},{4,4},{5,5},{6,36},{7,37},{8,8},{9,9},{1... | collective-permute-start | bytes 405512 | tf_op jit(solution)/shard_map/ppermute | solution.py:303
  73.0 1.5 %collective-permute-start.2 = (f32[264,128]{1,0:T(8,128)}, f32[264,128]{1,0:T(8,128)S(1)}, u32[]{:S(2)}, u32[]{:S(2)}) collective-permute-start(f32[264,128]{1,0:T(8,128)} %get-tuple-element.13), channel_id=1, source_target_pairs={{0,4},{1,5},{2,36},{3,37},{4,0},{5,1},{6,32},{7,33},{8,12},{9,13},... | collective-permute-start | bytes 405512 | tf_op jit(solution)/shard_map/ppermute | solution.py:303
  74.6 0.0 collective-permute-start.3
  74.6 7.4 %collective-permute-start.4 = (f32[264,128]{1,0:T(8,128)S(1)}, f32[264,128]{1,0:T(8,128)S(1)}, u32[]{:S(2)}, u32[]{:S(2)}) collective-permute-start(f32[264,128]{1,0:T(8,128)S(1)} %get-tuple-element.15), channel_id=1, source_target_pairs={{0,36},{1,37},{2,4},{3,5},{4,32},{5,33},{6,0},{7,1},{8,44},{9,45},... | collective-permute-start | bytes 405512 | tf_op jit(solution)/shard_map/ppermute | solution.py:303
  82.0 9.6 %collective-permute-done.1.refs_0_ = f32[264,128]{1,0:T(8,128)S(1)} collective-permute-done((f32[264,128]{1,0:T(8,128)}, f32[264,128]{1,0:T(8,128)S(1)}, u32[]{:S(2)}, u32[]{:S(2)}) %collective-permute-start.1) | collective-permute-done | bytes 135200 | tf_op jit(solution)/shard_map/ppermute | solution.py:303
  91.6 0.0 collective-permute-done.2.refs_1_
  91.6 5.3 %collective-permute-done.3.refs_2_ = f32[264,128]{1,0:T(8,128)S(1)} collective-permute-done((f32[264,128]{1,0:T(8,128)}, f32[264,128]{1,0:T(8,128)S(1)}, u32[]{:S(2)}, u32[]{:S(2)}) %collective-permute-start.3) | collective-permute-done | bytes 135200 | tf_op jit(solution)/shard_map/ppermute | solution.py:303
  96.9 0.0 collective-permute-done.4.refs_3_
  96.9 6.7 %solved_blocks.1 = (f32[1,128,128]{2,1,0:T(8,128)}, f32[1,128,128]{2,1,0:T(8,128)}) custom-call(s32[1]{0:T(128)} %bitcast.last_ref, f32[264,128]{1,0:T(8,128)S(1)} %collective-permute-done.1.refs_0_, f32[264,128]{1,0:T(8,128)S(1)} %collective-permute-done.2.refs_1_, f32[264,128]{1,0:T(8,128)S(1)} %collective-permute-done.3.refs_2_, ...), custom_call_target="tpu_custom_call" | custom-call | flops 10000000 | bytes 786432 | tf_op jit(solution)/shard_map/solved_blocks/pallas_call | solution.py:273
Async XLA Ops:
  0.6 4.0 %copy-start.4 = (f32[2]{0:T(128)S(1)}, f32[2]{0:T(128)}, u32[]{:S(2)}) copy-start(f32[2]{0:T(128)} %damping_ref.3) | copy-start | bytes 28
  5.6 1.2 %copy-start.1 = (bf16[16,49,8,128]{3,2,1,0:T(8,128)(2,1)}, bf16[16,49,8,128]{3,2,1,0:T(8,128)(2,1)S(1)}, u32[]{:S(2)}) copy-start(bf16[16,49,8,128]{3,2,1,0:T(8,128)(2,1)S(1)} %sent_columns.2) | copy-start | bytes 4816900
  6.8 29.1 %all-to-all-start = ((bf16[16,392,128]{2,1,0:T(8,128)(2,1)}), bf16[16,392,128]{2,1,0:T(8,128)(2,1)}, u32[]{:S(2)}, u32[]{:S(2)}) async-start(bf16[16,392,128]{2,1,0:T(8,128)(2,1)} %bitcast.13), calls=%async_computation | async-start | bytes 3211264 | tf_op jit(solution)/shard_map/all_to_all | solution.py:295
  14.7 1.1 %copy-start = (bf16[16,49,8,128]{3,2,1,0:T(8,128)(2,1)}, bf16[16,49,8,128]{3,2,1,0:T(8,128)(2,1)S(1)}, u32[]{:S(2)}) copy-start(bf16[16,49,8,128]{3,2,1,0:T(8,128)(2,1)S(1)} %sent_columns.3) | copy-start | bytes 4816900
  35.9 26.1 %all-to-all-start.1 = ((bf16[16,392,128]{2,1,0:T(8,128)(2,1)}), bf16[16,392,128]{2,1,0:T(8,128)(2,1)S(1)}, u32[]{:S(2)}, u32[]{:S(2)}) async-start(bf16[16,392,128]{2,1,0:T(8,128)(2,1)} %bitcast.12), calls=%async_computation.1 | async-start | bytes 3211264 | tf_op jit(solution)/shard_map/all_to_all | solution.py:295
  42.2 20.5 %collective-permute-start = (bf16[16,392,128]{2,1,0:T(8,128)(2,1)}, bf16[16,392,128]{2,1,0:T(8,128)(2,1)S(1)}, u32[]{:S(2)}, u32[]{:S(2)}) collective-permute-start(bf16[16,392,128]{2,1,0:T(8,128)(2,1)} %all-to-all-done.x_ref), channel_id=1, source_target_pairs={{64,0},{65,1},{66,2},{67,3},{68,4},{69,5},{70,6},{71,7},{72,8},{73... | collective-permute-start | bytes 4816904 | tf_op jit(solution)/shard_map/ppermute | solution.py:298
  46.3 1.2 %copy-start.2 = (bf16[2,3072,128]{2,1,0:T(8,128)(2,1)}, bf16[2,3072,128]{2,1,0:T(8,128)(2,1)S(1)}, u32[]{:S(2)}) copy-start(bf16[2,3072,128]{2,1,0:T(8,128)(2,1)S(1)} %get-tuple-element.11.x0_ref) | copy-start | bytes 4718596
  62.7 1.4 %copy-start.3 = (bf16[2,3072,128]{2,1,0:T(8,128)(2,1)S(1)}, bf16[2,3072,128]{2,1,0:T(8,128)(2,1)}, u32[]{:S(2)}) copy-start(bf16[2,3072,128]{2,1,0:T(8,128)(2,1)} %copy-done.2) | copy-start | bytes 4718596
  67.3 24.4 %collective-permute-start.1 = (f32[264,128]{1,0:T(8,128)}, f32[264,128]{1,0:T(8,128)S(1)}, u32[]{:S(2)}, u32[]{:S(2)}) collective-permute-start(f32[264,128]{1,0:T(8,128)} %get-tuple-element.12), channel_id=1, source_target_pairs={{0,0},{1,1},{2,32},{3,33},{4,4},{5,5},{6,36},{7,37},{8,8},{9,9},{1... | collective-permute-start | bytes 405512 | tf_op jit(solution)/shard_map/ppermute | solution.py:303
  73.0 18.6 %collective-permute-start.2 = (f32[264,128]{1,0:T(8,128)}, f32[264,128]{1,0:T(8,128)S(1)}, u32[]{:S(2)}, u32[]{:S(2)}) collective-permute-start(f32[264,128]{1,0:T(8,128)} %get-tuple-element.13), channel_id=1, source_target_pairs={{0,4},{1,5},{2,36},{3,37},{4,0},{5,1},{6,32},{7,33},{8,12},{9,13},... | collective-permute-start | bytes 405512 | tf_op jit(solution)/shard_map/ppermute | solution.py:303
  74.6 22.4 %collective-permute-start.3 = (f32[264,128]{1,0:T(8,128)}, f32[264,128]{1,0:T(8,128)S(1)}, u32[]{:S(2)}, u32[]{:S(2)}) collective-permute-start(f32[264,128]{1,0:T(8,128)} %get-tuple-element.14), channel_id=1, source_target_pairs={{0,32},{1,33},{2,0},{3,1},{4,36},{5,37},{6,4},{7,5},{8,40},{9,41},... | collective-permute-start | bytes 405512 | tf_op jit(solution)/shard_map/ppermute | solution.py:303
  74.6 22.4 %collective-permute-start.4 = (f32[264,128]{1,0:T(8,128)S(1)}, f32[264,128]{1,0:T(8,128)S(1)}, u32[]{:S(2)}, u32[]{:S(2)}) collective-permute-start(f32[264,128]{1,0:T(8,128)S(1)} %get-tuple-element.15), channel_id=1, source_target_pairs={{0,36},{1,37},{2,4},{3,5},{4,32},{5,33},{6,0},{7,1},{8,44},{9,45},... | collective-permute-start | bytes 405512 | tf_op jit(solution)/shard_map/ppermute | solution.py:303

commit v4 on v3

--- a/solution.py
+++ b/solution.py
@@ -23,6 +23,15 @@
 
 
 BITS = [tuple((d >> s) & 1 for s in (5, 4, 3, 2, 1, 0)) for d in range(64)]
+
+
+Y_OF = {(0, 0): 1, (0, 1): 3, (1, 0): 2, (1, 1): 0}
+CODE_OF = {y: code for code, y in Y_OF.items()}
+
+
+def member_index(m, turn, z2, z1):
+    y = Y_OF[((m >> 2) & 1, m >> 3)]
+    return dp_index(y >> 1, y & 1, ((m >> 1) & 1) ^ turn, z2, z1, m & 1)
 
 
 def column_groups():
@@ -32,7 +41,7 @@
             for z1 in range(2):
                 groups.append(
                     [
-                        section * 64 + dp_index(m >> 3, (m >> 2) & 1, ((m >> 1) & 1) ^ flipped(section), z2, z1, m & 1)
+                        section * 64 + member_index(m, flipped(section), z2, z1)
                         for m in range(16)
                     ]
                 )
@@ -53,7 +62,9 @@
     for section in range(4):
         turn = flipped(section)
         for d, (y1, y0, xl, z2, z1, z0) in enumerate(BITS):
-            route.append((section * 64 + d, section * 64 + dp_index(z1 ^ a, y0, xl ^ turn, z2 ^ b, y1, z0)))
+            home_y0, home_z1 = CODE_OF[y1 * 2 + y0]
+            home = dp_index(z1 ^ a, home_y0, xl ^ turn, z2 ^ b, home_z1, z0)
+            route.append((section * 64 + d, section * 64 + home))
     return route
 
 
@@ -127,14 +138,13 @@
     return lax.dot_general(left, right, (((0,), (0,)), ((), ())), preferred_element_type=jnp.float32)
 
 
-def own_kernel(x_ref, gram_ref, level_ref, kept_ref):
+def own_kernel(x_ref, gram_ref, level_ref):
     squares, damping = level_rows(x_ref)
     level_ref[0:1, :] = squares
     level_ref[1:2, :] = damping
     level_ref[2:PANEL, :] = jnp.zeros((PANEL - 2, B), jnp.float32)
     for zz in range(2):
         x = tokens_of(x_ref, zz)
-        kept_ref[zz] = x
         gram_ref[zz] = gram(x, x)
 
 
@@ -145,27 +155,32 @@
         out_shape=[
             jax.ShapeDtypeStruct((2, B, B), jnp.float32),
             jax.ShapeDtypeStruct((PANEL, B), jnp.float32),
-            jax.ShapeDtypeStruct((2, x.shape[0] * (x.shape[1] - PANEL) // 2, B), jnp.bfloat16),
         ],
         in_specs=[vmem],
-        out_specs=[vmem] * 3,
+        out_specs=[vmem] * 2,
         name="own_grams",
         cost_estimate=pl.CostEstimate(flops=4 * 3072 * B * B, bytes_accessed=2 * 3072 * B * 2, transcendentals=0),
-        compiler_params=pltpu.CompilerParams(vmem_limit_bytes=16 * 2**20),
+        compiler_params=pltpu.CompilerParams(vmem_limit_bytes=8 * 2**20),
     )(x)
 
 
-def gram_kernel(pos_ref, d0_ref, level_ref, x0_ref, x1_ref, x2_ref, *out_refs):
+def gram_kernel(pos_ref, d0_ref, level_ref, x0_ref, x1_ref, x2_ref, *refs):
+    out_refs, (held_ref, sem) = refs[:4], refs[4:]
     turn, z2, z1 = pos_ref[0], pos_ref[1], pos_ref[2]
+    copy = pltpu.make_async_copy(x0_ref, held_ref, sem)
+    copy.start()
     row = lax.broadcasted_iota(jnp.int32, (B, B), 0)
     col = lax.broadcasted_iota(jnp.int32, (B, B), 1)
-    levels = [(level_ref[0:1, :], level_ref[1:2, :])] + [level_rows(x_ref) for x_ref in (x1_ref, x2_ref)]
+    afters = []
     for zz in range(2):
-        x0, x1, x2 = x0_ref[zz], tokens_of(x1_ref, zz), tokens_of(x2_ref, zz, turn)
-        middle = gram(x1, jnp.concatenate([x1, x2], axis=1))
-        d0, d1, c12 = d0_ref[zz], middle[:, :B], middle[:, B:]
-        c01 = gram(x1, x0).T
-        d2 = gram(x2, x2)
+        x1, x2 = tokens_of(x1_ref, zz), tokens_of(x2_ref, zz, turn)
+        afters.append(gram(x2, jnp.concatenate([x1, x2], axis=1)))
+    levels = [(level_ref[0:1, :], level_ref[1:2, :]), level_rows(x1_ref), level_rows(x2_ref)]
+    copy.wait()
+    for zz in range(2):
+        x0, x1 = tokens_of(held_ref, zz), tokens_of(x1_ref, zz)
+        first, after = gram(x1, jnp.concatenate([x0, x1], axis=1)), afters[zz]
+        c01, d1, c12, d2, d0 = first[:, :B], first[:, B:], after[:, :B], after[:, B:], d0_ref[zz]
         for layer, (d, n, c) in enumerate(((d0, d1, c01), (d1, d2, c12))):
             packed = jnp.where(row >= col, d, n)
             edge = jnp.sum(jnp.where(row == col, n, 0.0), axis=0, keepdims=True)
@@ -189,11 +204,15 @@
     return pl.pallas_call(
         gram_kernel,
         out_shape=[jax.ShapeDtypeStruct((2 * B + PANEL, B), jnp.float32)] * 4,
-        in_specs=[pl.BlockSpec(memory_space=pltpu.SMEM)] + [vmem] * 5,
+        in_specs=[pl.BlockSpec(memory_space=pltpu.SMEM)]
+        + [vmem] * 2
+        + [pl.BlockSpec(memory_space=pltpu.MemorySpace.HBM)]
+        + [vmem] * 2,
         out_specs=[vmem] * 4,
+        scratch_shapes=[pltpu.VMEM(x0.shape, jnp.bfloat16), pltpu.SemaphoreType.DMA(())],
         name="partial_grams",
         cost_estimate=pl.CostEstimate(flops=8 * 3072 * B * B * 2, bytes_accessed=6 * 3072 * B * 2, transcendentals=0),
-        compiler_params=pltpu.CompilerParams(vmem_limit_bytes=24 * 2**20),
+        compiler_params=pltpu.CompilerParams(vmem_limit_bytes=16 * 2**20),
     )(position, d0, level0, x0, x1, x2)
 
 
@@ -255,7 +274,7 @@
     following = jnp.where(row == col, diagonal, jnp.where(row < col, packed, turned))
     final = last_ref[0] == 1
     following = jnp.where(final, jnp.where(row == col, 1.0, 0.0), following)
-    cross = jnp.where(final, 0.0, owned[:B] / tokens)
+    cross = jnp.where(final, 0.0, owned[:B].T / tokens)
     solved = jnp.concatenate(inverted(cut_panels(following)), axis=0)
     coupling = jnp.dot(cross, solved, precision=lax.Precision.HIGHEST, preferred_element_type=jnp.float32)
     coupling_ref[0] = coupling
@@ -298,8 +317,8 @@
     x2 = lax.ppermute(x0, EVERY, following_route())
     x1 = exchanged(sent_columns(by_layer, damping, 1))
     position = jnp.stack([section == 1, (dp >> 2) & 1, (dp >> 1) & 1]).astype(jnp.int32)
-    d0, level0, kept = own_grams(x0)
-    sent = partial_grams(d0, level0, kept, x1, x2, position)
+    d0, level0 = own_grams(x0)
+    sent = partial_grams(d0, level0, x0, x1, x2, position)
     arrived = [lax.ppermute(sent[a * 2 + b], EVERY, home_route(a, b)) for a in range(2) for b in range(2)]
     last = jnp.logical_and(section == section_count - 1, dp // (group_size // local_layers) == local_layers - 1)
     return tuple(solved_blocks(arrived, last.astype(jnp.int32)[None], token_rows * group_size, model_width))

time: 104 us -> 101 us (0.971)
  the two profiles are of different devices: /device:TPU:228 before, /device:TPU:1 now
where the time goes in v4:
time: 101 us
  waiting for transfers between devices  51.2 us (51%)
  starting transfers between devices  27.5 us (27%)
  Pallas kernels  15.1 us (15%)
  local copies, waits for them, and re-layouts  6.29 us (6%)
    all_to_all x2, waiting for transfers between devices, exchanged(): lax.all_to_all(columns, EVERY, split_axis=0, concat_axis=0, axis_index_gr...  35.3 us
    ppermute x4, waiting for transfers between devices, local(): lax.ppermute(sent[a * 2 + b], EVERY, home_route(a, b))  12.1 us
    ppermute x4, starting transfers between devices, local(): lax.ppermute(sent[a * 2 + b], EVERY, home_route(a, b))  12 us
    all_to_all x2, starting transfers between devices, exchanged(): lax.all_to_all(columns, EVERY, split_axis=0, concat_axis=0, axis_index_gr...  11.8 us
    pallas_call x1, Pallas kernels, solved_blocks(): pl.pallas_call(partial(solve_kernel, float(tokens), float(width)), out_sh...  6.69 us
    pallas_call x1, Pallas kernels, partial_grams(): pl.pallas_call(gram_kernel, out_shape=[jax.ShapeDtypeStruct((2 * B + PANE...  4.39 us
    reshape x1, local copies, waits for them, and re-layouts, local(): activations.reshape(token_rows // PANEL, PANEL, local_layers, model_width)  3.97 us
    ppermute x1, waiting for transfers between devices, local(): x2 = lax.ppermute(x0, EVERY, following_route())  3.83 us
  transfers between devices with their start and end apart: 7, of which 6 were waited for; matrix products, arithmetic and copies ran while one was open for 0% of the time, Pallas kernels for 3%

profile of v4, /device:TPU:1, one launch (start us, length us, event | category | flops | bytes accessed | tf_op | source)
XLA Modules:
  0.0 100.9 jit_solution(11780437742581508864)
XLA Ops:
  0.6 0.0 copy-start.2
  0.6 4.0 %copy.9 = bf16[24,8,2,4096]{3,1,2,0:T(8,128)(2,1)S(1)} copy(bf16[24,8,2,4096]{3,2,1,0:T(2,128)(2,1)} %bitcast.14) | data formatting | bytes 6291456 | tf_op jit(solution)/shard_map/reshape | solution.py:310
  4.6 0.0 copy-done.2
  4.6 1.0 %sent_columns.2 = bf16[16,49,8,128]{3,2,1,0:T(8,128)(2,1)S(1)} custom-call(f32[2]{0:T(128)S(1)} %copy-done.2, bf16[24,2,8,4096]{3,2,1,0:T(8,128)(2,1)S(1)} %bitcast.10), custom_call_target="tpu_custom_call" | custom-call | flops 2097152 | bytes 4194304 | tf_op jit(solution)/shard_map/sent_columns/pallas_call | solution.py:109
  5.6 0.0 copy-start.1
  5.7 1.2 %copy-done.1 = bf16[16,49,8,128]{3,2,1,0:T(8,128)(2,1)} copy-done((bf16[16,49,8,128]{3,2,1,0:T(8,128)(2,1)}, bf16[16,49,8,128]{3,2,1,0:T(8,128)(2,1)S(1)}, u32[]{:S(2)}) %copy-start.1) | copy-done | bytes 1605656
  6.8 7.7 %all-to-all-start = ((bf16[16,392,128]{2,1,0:T(8,128)(2,1)}), bf16[16,392,128]{2,1,0:T(8,128)(2,1)}, u32[]{:S(2)}, u32[]{:S(2)}) async-start(bf16[16,392,128]{2,1,0:T(8,128)(2,1)} %bitcast.13), calls=%async_computation | async-start | bytes 3211264 | tf_op jit(solution)/shard_map/all_to_all | solution.py:314
  14.5 1.0 %sent_columns.3 = bf16[16,49,8,128]{3,2,1,0:T(8,128)(2,1)S(1)} custom-call(f32[2]{0:T(128)S(1)} %copy-done.2, bf16[24,2,8,4096]{3,2,1,0:T(8,128)(2,1)S(1)} %bitcast.11), custom_call_target="tpu_custom_call" | custom-call | flops 2097152 | bytes 4194304 | tf_op jit(solution)/shard_map/sent_columns/pallas_call | solution.py:109
  15.5 0.0 copy-start
  15.5 1.1 %copy-done = bf16[16,49,8,128]{3,2,1,0:T(8,128)(2,1)} copy-done((bf16[16,49,8,128]{3,2,1,0:T(8,128)(2,1)}, bf16[16,49,8,128]{3,2,1,0:T(8,128)(2,1)S(1)}, u32[]{:S(2)}) %copy-start) | copy-done | bytes 1605656
  16.7 20.9 %all-to-all-done.x_ref.x0_ref = bf16[16,392,128]{2,1,0:T(8,128)(2,1)} async-done(((bf16[16,392,128]{2,1,0:T(8,128)(2,1)}), bf16[16,392,128]{2,1,0:T(8,128)(2,1)}, u32[]{:S(2)}, u32[]{:S(2)}) %all-to-all-start) | async-done | bytes 1605664 | tf_op jit(solution)/shard_map/all_to_all | solution.py:314
  37.6 4.1 %all-to-all-start.1 = ((bf16[16,392,128]{2,1,0:T(8,128)(2,1)}), bf16[16,392,128]{2,1,0:T(8,128)(2,1)S(1)}, u32[]{:S(2)}, u32[]{:S(2)}) async-start(bf16[16,392,128]{2,1,0:T(8,128)(2,1)} %bitcast.12), calls=%async_computation.1 | async-start | bytes 3211264 | tf_op jit(solution)/shard_map/all_to_all | solution.py:314
  41.7 3.7 %collective-permute-start = (bf16[16,392,128]{2,1,0:T(8,128)(2,1)}, bf16[16,392,128]{2,1,0:T(8,128)(2,1)S(1)}, u32[]{:S(2)}, u32[]{:S(2)}) collective-permute-start(bf16[16,392,128]{2,1,0:T(8,128)(2,1)} %all-to-all-done.x_ref.x0_ref), channel_id=1, source_target_pairs={{64,0},{65,1},{66,2},{67,3},{68,4},{69,5},{70,6},{71,7},{72,8},{73... | collective-permute-start | bytes 4816904 | tf_op jit(solution)/shard_map/ppermute | solution.py:317
  45.5 0.1 pad_add_fusion.pos_ref
  45.5 2.0 %own_grams.1 = (f32[2,128,128]{2,1,0:T(8,128)S(1)}, f32[8,128]{1,0:T(8,128)S(1)}) custom-call(bf16[16,392,128]{2,1,0:T(8,128)(2,1)} %all-to-all-done.x_ref.x0_ref), custom_call_target="tpu_custom_call" | custom-call | flops 201326592 | bytes 1572864 | tf_op jit(solution)/shard_map/own_grams/pallas_call | solution.py:153
  47.6 14.4 %all-to-all-done.1.x1_ref = bf16[16,392,128]{2,1,0:T(8,128)(2,1)S(1)} async-done(((bf16[16,392,128]{2,1,0:T(8,128)(2,1)}), bf16[16,392,128]{2,1,0:T(8,128)(2,1)S(1)}, u32[]{:S(2)}, u32[]{:S(2)}) %all-to-all-start.1) | async-done | bytes 1605664 | tf_op jit(solution)/shard_map/all_to_all | solution.py:314
  62.0 3.8 %collective-permute-done.x2_ref = bf16[16,392,128]{2,1,0:T(8,128)(2,1)S(1)} collective-permute-done((bf16[16,392,128]{2,1,0:T(8,128)(2,1)}, bf16[16,392,128]{2,1,0:T(8,128)(2,1)S(1)}, u32[]{:S(2)}, u32[]{:S(2)}) %collective-permute-start) | collective-permute-done | bytes 1605664 | tf_op jit(solution)/shard_map/ppermute | solution.py:317
  65.8 4.4 %partial_grams.1 = (f32[264,128]{1,0:T(8,128)}, f32[264,128]{1,0:T(8,128)}, f32[264,128]{1,0:T(8,128)}, f32[264,128]{1,0:T(8,128)S(1)}) custom-call(s32[3]{0:T(128)S(1)} %pad_add_fusion.pos_ref, f32[2,128,128]{2,1,0:T(8,128)S(1)} %get-tuple-element.8.d0_ref, f32[8,128]{1,0:T(8,128)S(1)} %get-tuple-element.9.level_ref, ...), custom_call_target="tpu_custom_call" | custom-call | flops 805306368 | bytes 4718592 | tf_op jit(solution)/shard_map/partial_grams/pallas_call | solution.py:204
  70.2 2.6 %collective-permute-start.1 = (f32[264,128]{1,0:T(8,128)}, f32[264,128]{1,0:T(8,128)S(1)}, u32[]{:S(2)}, u32[]{:S(2)}) collective-permute-start(f32[264,128]{1,0:T(8,128)} %get-tuple-element.10), channel_id=1, source_target_pairs={{0,18},{1,19},{2,50},{3,51},{4,22},{5,23},{6,54},{7,55},{8,26},{9,... | collective-permute-start | bytes 405512 | tf_op jit(solution)/shard_map/ppermute | solution.py:322
  72.8 5.1 %collective-permute-start.2 = (f32[264,128]{1,0:T(8,128)}, f32[264,128]{1,0:T(8,128)S(1)}, u32[]{:S(2)}, u32[]{:S(2)}) collective-permute-start(f32[264,128]{1,0:T(8,128)} %get-tuple-element.11), channel_id=1, source_target_pairs={{0,22},{1,23},{2,54},{3,55},{4,18},{5,19},{6,50},{7,51},{8,30},{9,... | collective-permute-start | bytes 405512 | tf_op jit(solution)/shard_map/ppermute | solution.py:322
  77.9 4.2 %collective-permute-start.3 = (f32[264,128]{1,0:T(8,128)}, f32[264,128]{1,0:T(8,128)S(1)}, u32[]{:S(2)}, u32[]{:S(2)}) collective-permute-start(f32[264,128]{1,0:T(8,128)} %get-tuple-element.12), channel_id=1, source_target_pairs={{0,50},{1,51},{2,18},{3,19},{4,54},{5,55},{6,22},{7,23},{8,58},{9,... | collective-permute-start | bytes 405512 | tf_op jit(solution)/shard_map/ppermute | solution.py:322
  82.2 0.0 collective-permute-start.4
  82.2 0.0 collective-permute-done.1.refs_0_
  82.2 9.6 %collective-permute-done.2.refs_1_ = f32[264,128]{1,0:T(8,128)S(1)} collective-permute-done((f32[264,128]{1,0:T(8,128)}, f32[264,128]{1,0:T(8,128)S(1)}, u32[]{:S(2)}, u32[]{:S(2)}) %collective-permute-start.2) | collective-permute-done | bytes 135200 | tf_op jit(solution)/shard_map/ppermute | solution.py:322
  91.8 1.1 %collective-permute-done.3.refs_2_ = f32[264,128]{1,0:T(8,128)S(1)} collective-permute-done((f32[264,128]{1,0:T(8,128)}, f32[264,128]{1,0:T(8,128)S(1)}, u32[]{:S(2)}, u32[]{:S(2)}) %collective-permute-start.3) | collective-permute-done | bytes 135200 | tf_op jit(solution)/shard_map/ppermute | solution.py:322
  92.9 1.3 %collective-permute-done.4.refs_3_ = f32[264,128]{1,0:T(8,128)S(1)} collective-permute-done((f32[264,128]{1,0:T(8,128)S(1)}, f32[264,128]{1,0:T(8,128)S(1)}, u32[]{:S(2)}, u32[]{:S(2)}) %collective-permute-start.4) | collective-permute-done | bytes 135200 | tf_op jit(solution)/shard_map/ppermute | solution.py:322
  94.2 6.7 %solved_blocks.1 = (f32[1,128,128]{2,1,0:T(8,128)}, f32[1,128,128]{2,1,0:T(8,128)}) custom-call(s32[1]{0:T(128)} %bitcast.last_ref, f32[264,128]{1,0:T(8,128)S(1)} %collective-permute-done.1.refs_0_, f32[264,128]{1,0:T(8,128)S(1)} %collective-permute-done.2.refs_1_, f32[264,128]{1,0:T(8,128)S(1)} %collective-permute-done.3.refs_2_, ...), custom_call_target="tpu_custom_call" | custom-call | flops 10000000 | bytes 786432 | tf_op jit(solution)/shard_map/solved_blocks/pallas_call | solution.py:292
Async XLA Ops:
  0.6 4.0 %copy-start.2 = (f32[2]{0:T(128)S(1)}, f32[2]{0:T(128)}, u32[]{:S(2)}) copy-start(f32[2]{0:T(128)} %damping_ref.3) | copy-start | bytes 28
  5.6 1.2 %copy-start.1 = (bf16[16,49,8,128]{3,2,1,0:T(8,128)(2,1)}, bf16[16,49,8,128]{3,2,1,0:T(8,128)(2,1)S(1)}, u32[]{:S(2)}) copy-start(bf16[16,49,8,128]{3,2,1,0:T(8,128)(2,1)S(1)} %sent_columns.2) | copy-start | bytes 4816900
  6.8 30.8 %all-to-all-start = ((bf16[16,392,128]{2,1,0:T(8,128)(2,1)}), bf16[16,392,128]{2,1,0:T(8,128)(2,1)}, u32[]{:S(2)}, u32[]{:S(2)}) async-start(bf16[16,392,128]{2,1,0:T(8,128)(2,1)} %bitcast.13), calls=%async_computation | async-start | bytes 3211264 | tf_op jit(solution)/shard_map/all_to_all | solution.py:314
  15.5 1.2 %copy-start = (bf16[16,49,8,128]{3,2,1,0:T(8,128)(2,1)}, bf16[16,49,8,128]{3,2,1,0:T(8,128)(2,1)S(1)}, u32[]{:S(2)}) copy-start(bf16[16,49,8,128]{3,2,1,0:T(8,128)(2,1)S(1)} %sent_columns.3) | copy-start | bytes 4816900
  37.6 24.4 %all-to-all-start.1 = ((bf16[16,392,128]{2,1,0:T(8,128)(2,1)}), bf16[16,392,128]{2,1,0:T(8,128)(2,1)S(1)}, u32[]{:S(2)}, u32[]{:S(2)}) async-start(bf16[16,392,128]{2,1,0:T(8,128)(2,1)} %bitcast.12), calls=%async_computation.1 | async-start | bytes 3211264 | tf_op jit(solution)/shard_map/all_to_all | solution.py:314
  41.7 24.1 %collective-permute-start = (bf16[16,392,128]{2,1,0:T(8,128)(2,1)}, bf16[16,392,128]{2,1,0:T(8,128)(2,1)S(1)}, u32[]{:S(2)}, u32[]{:S(2)}) collective-permute-start(bf16[16,392,128]{2,1,0:T(8,128)(2,1)} %all-to-all-done.x_ref.x0_ref), channel_id=1, source_target_pairs={{64,0},{65,1},{66,2},{67,3},{68,4},{69,5},{70,6},{71,7},{72,8},{73... | collective-permute-start | bytes 4816904 | tf_op jit(solution)/shard_map/ppermute | solution.py:317
  70.2 12.0 %collective-permute-start.1 = (f32[264,128]{1,0:T(8,128)}, f32[264,128]{1,0:T(8,128)S(1)}, u32[]{:S(2)}, u32[]{:S(2)}) collective-permute-start(f32[264,128]{1,0:T(8,128)} %get-tuple-element.10), channel_id=1, source_target_pairs={{0,18},{1,19},{2,50},{3,51},{4,22},{5,23},{6,54},{7,55},{8,26},{9,... | collective-permute-start | bytes 405512 | tf_op jit(solution)/shard_map/ppermute | solution.py:322
  72.8 19.0 %collective-permute-start.2 = (f32[264,128]{1,0:T(8,128)}, f32[264,128]{1,0:T(8,128)S(1)}, u32[]{:S(2)}, u32[]{:S(2)}) collective-permute-start(f32[264,128]{1,0:T(8,128)} %get-tuple-element.11), channel_id=1, source_target_pairs={{0,22},{1,23},{2,54},{3,55},{4,18},{5,19},{6,50},{7,51},{8,30},{9,... | collective-permute-start | bytes 405512 | tf_op jit(solution)/shard_map/ppermute | solution.py:322
  77.9 15.0 %collective-permute-start.3 = (f32[264,128]{1,0:T(8,128)}, f32[264,128]{1,0:T(8,128)S(1)}, u32[]{:S(2)}, u32[]{:S(2)}) collective-permute-start(f32[264,128]{1,0:T(8,128)} %get-tuple-element.12), channel_id=1, source_target_pairs={{0,50},{1,51},{2,18},{3,19},{4,54},{5,55},{6,22},{7,23},{8,58},{9,... | collective-permute-start | bytes 405512 | tf_op jit(solution)/shard_map/ppermute | solution.py:322
  82.2 12.1 %collective-permute-start.4 = (f32[264,128]{1,0:T(8,128)S(1)}, f32[264,128]{1,0:T(8,128)S(1)}, u32[]{:S(2)}, u32[]{:S(2)}) collective-permute-start(f32[264,128]{1,0:T(8,128)S(1)} %get-tuple-element.13), channel_id=1, source_target_pairs={{0,54},{1,55},{2,22},{3,23},{4,50},{5,51},{6,18},{7,19},{8,62},{9,... | collective-permute-start | bytes 405512 | tf_op jit(solution)/shard_map/ppermute | solution.py:322

commit v5 on v4

--- a/solution.py
+++ b/solution.py
@@ -238,19 +238,20 @@
                 own[q] = jnp.where(sub == j, top, own[q] - own[j] * top)
             top = panel[j : j + 1, :] * scale
             panel = jnp.where(sub == j, top, panel - own[j] * top)
-        following = k + 1 if k + 1 < count else None
-        rows = [i for i in range(count) if i != k and i != following]
-        left = jnp.concatenate([jnp.where(here, panels[i], 0.0) for i in rows], axis=0)
-        right = jnp.concatenate([panel if i == k else nothing for i in range(count)], axis=0)
-        product = jnp.dot(left, right, precision=lax.Precision.HIGHEST, preferred_element_type=jnp.float32)
-        for at, i in enumerate(rows):
-            panels[i] = jnp.where(here, 0.0, panels[i]) - product[at * STEP : (at + 1) * STEP]
-        if following is not None:
-            coefs = spread(panels[following], first)
-            rest = jnp.where(here, 0.0, panels[following])
+        close = [i for i in range(k + 1, min(k + 1 + 1, count))]
+        rows = [i for i in range(count) if i != k and i not in close]
+        coefs = [spread(panels[i], first) for i in close]
+        for i, weights in zip(close, coefs):
+            rest = jnp.where(here, 0.0, panels[i])
             for j in range(STEP):
-                rest = rest - coefs[j] * panel[j : j + 1, :]
-            panels[following] = rest
+                rest = rest - weights[j] * panel[j : j + 1, :]
+            panels[i] = rest
+        if rows:
+            left = jnp.concatenate([jnp.where(here, panels[i], 0.0) for i in rows], axis=0)
+            right = jnp.concatenate([panel if i == k else nothing for i in range(count)], axis=0)
+            product = jnp.dot(left, right, precision=lax.Precision.HIGHEST, preferred_element_type=jnp.float32)
+            for at, i in enumerate(rows):
+                panels[i] = jnp.where(here, 0.0, panels[i]) - product[at * STEP : (at + 1) * STEP]
         panels[k] = panel
     return panels
 
@@ -282,7 +283,6 @@
         coupling, cross, (((1,), (1,)), ((), ())), precision=lax.Precision.HIGHEST, preferred_element_type=jnp.float32
     )
     schur = damped - product
-    schur = (schur + schur.T) * 0.5
     for i, panel in enumerate(inverted(cut_panels(schur))):
         inverse_ref[0, i * STEP : (i + 1) * STEP, :] = panel
 

time: 101 us -> 101 us (level)
  no operation moved by 1% of the time
where the time goes in v5:
time: 101 us
  waiting for transfers between devices  51.2 us (51%)
  starting transfers between devices  27.5 us (27%)
  Pallas kernels  15.1 us (15%)
  local copies, waits for them, and re-layouts  6.29 us (6%)
    all_to_all x2, waiting for transfers between devices, exchanged(): lax.all_to_all(columns, EVERY, split_axis=0, concat_axis=0, axis_index_gr...  35.3 us
    ppermute x4, waiting for transfers between devices, local(): lax.ppermute(sent[a * 2 + b], EVERY, home_route(a, b))  12.1 us
    ppermute x4, starting transfers between devices, local(): lax.ppermute(sent[a * 2 + b], EVERY, home_route(a, b))  12 us
    all_to_all x2, starting transfers between devices, exchanged(): lax.all_to_all(columns, EVERY, split_axis=0, concat_axis=0, axis_index_gr...  11.8 us
    pallas_call x1, Pallas kernels, solved_blocks(): pl.pallas_call(partial(solve_kernel, float(tokens), float(width)), out_sh...  6.64 us
    pallas_call x1, Pallas kernels, partial_grams(): pl.pallas_call(gram_kernel, out_shape=[jax.ShapeDtypeStruct((2 * B + PANE...  4.39 us
    reshape x1, local copies, waits for them, and re-layouts, local(): activations.reshape(token_rows // PANEL, PANEL, local_layers, model_width)  3.97 us
    ppermute x1, waiting for transfers between devices, local(): x2 = lax.ppermute(x0, EVERY, following_route())  3.83 us
  transfers between devices with their start and end apart: 7, of which 6 were waited for; matrix products, arithmetic and copies ran while one was open for 0% of the time, Pallas kernels for 3%

profile of v5, /device:TPU:1, one launch (start us, length us, event | category | flops | bytes accessed | tf_op | source)
XLA Modules:
  0.0 100.9 jit_solution(15997916594677699317)
XLA Ops:
  0.6 0.0 copy-start.2
  0.6 4.0 %copy.9 = bf16[24,8,2,4096]{3,1,2,0:T(8,128)(2,1)S(1)} copy(bf16[24,8,2,4096]{3,2,1,0:T(2,128)(2,1)} %bitcast.14) | data formatting | bytes 6291456 | tf_op jit(solution)/shard_map/reshape | solution.py:310
  4.6 0.0 copy-done.2
  4.6 1.0 %sent_columns.2 = bf16[16,49,8,128]{3,2,1,0:T(8,128)(2,1)S(1)} custom-call(f32[2]{0:T(128)S(1)} %copy-done.2, bf16[24,2,8,4096]{3,2,1,0:T(8,128)(2,1)S(1)} %bitcast.10), custom_call_target="tpu_custom_call" | custom-call | flops 2097152 | bytes 4194304 | tf_op jit(solution)/shard_map/sent_columns/pallas_call | solution.py:109
  5.6 0.0 copy-start.1
  5.7 1.2 %copy-done.1 = bf16[16,49,8,128]{3,2,1,0:T(8,128)(2,1)} copy-done((bf16[16,49,8,128]{3,2,1,0:T(8,128)(2,1)}, bf16[16,49,8,128]{3,2,1,0:T(8,128)(2,1)S(1)}, u32[]{:S(2)}) %copy-start.1) | copy-done | bytes 1605656
  6.8 7.7 %all-to-all-start = ((bf16[16,392,128]{2,1,0:T(8,128)(2,1)}), bf16[16,392,128]{2,1,0:T(8,128)(2,1)}, u32[]{:S(2)}, u32[]{:S(2)}) async-start(bf16[16,392,128]{2,1,0:T(8,128)(2,1)} %bitcast.13), calls=%async_computation | async-start | bytes 3211264 | tf_op jit(solution)/shard_map/all_to_all | solution.py:314
  14.5 1.0 %sent_columns.3 = bf16[16,49,8,128]{3,2,1,0:T(8,128)(2,1)S(1)} custom-call(f32[2]{0:T(128)S(1)} %copy-done.2, bf16[24,2,8,4096]{3,2,1,0:T(8,128)(2,1)S(1)} %bitcast.11), custom_call_target="tpu_custom_call" | custom-call | flops 2097152 | bytes 4194304 | tf_op jit(solution)/shard_map/sent_columns/pallas_call | solution.py:109
  15.5 0.0 copy-start
  15.5 1.1 %copy-done = bf16[16,49,8,128]{3,2,1,0:T(8,128)(2,1)} copy-done((bf16[16,49,8,128]{3,2,1,0:T(8,128)(2,1)}, bf16[16,49,8,128]{3,2,1,0:T(8,128)(2,1)S(1)}, u32[]{:S(2)}) %copy-start) | copy-done | bytes 1605656
  16.7 20.9 %all-to-all-done.x_ref.x0_ref = bf16[16,392,128]{2,1,0:T(8,128)(2,1)} async-done(((bf16[16,392,128]{2,1,0:T(8,128)(2,1)}), bf16[16,392,128]{2,1,0:T(8,128)(2,1)}, u32[]{:S(2)}, u32[]{:S(2)}) %all-to-all-start) | async-done | bytes 1605664 | tf_op jit(solution)/shard_map/all_to_all | solution.py:314
  37.6 4.1 %all-to-all-start.1 = ((bf16[16,392,128]{2,1,0:T(8,128)(2,1)}), bf16[16,392,128]{2,1,0:T(8,128)(2,1)S(1)}, u32[]{:S(2)}, u32[]{:S(2)}) async-start(bf16[16,392,128]{2,1,0:T(8,128)(2,1)} %bitcast.12), calls=%async_computation.1 | async-start | bytes 3211264 | tf_op jit(solution)/shard_map/all_to_all | solution.py:314
  41.7 3.7 %collective-permute-start = (bf16[16,392,128]{2,1,0:T(8,128)(2,1)}, bf16[16,392,128]{2,1,0:T(8,128)(2,1)S(1)}, u32[]{:S(2)}, u32[]{:S(2)}) collective-permute-start(bf16[16,392,128]{2,1,0:T(8,128)(2,1)} %all-to-all-done.x_ref.x0_ref), channel_id=1, source_target_pairs={{64,0},{65,1},{66,2},{67,3},{68,4},{69,5},{70,6},{71,7},{72,8},{73... | collective-permute-start | bytes 4816904 | tf_op jit(solution)/shard_map/ppermute | solution.py:317
  45.5 0.1 pad_add_fusion.pos_ref
  45.5 2.0 %own_grams.1 = (f32[2,128,128]{2,1,0:T(8,128)S(1)}, f32[8,128]{1,0:T(8,128)S(1)}) custom-call(bf16[16,392,128]{2,1,0:T(8,128)(2,1)} %all-to-all-done.x_ref.x0_ref), custom_call_target="tpu_custom_call" | custom-call | flops 201326592 | bytes 1572864 | tf_op jit(solution)/shard_map/own_grams/pallas_call | solution.py:153
  47.6 14.4 %all-to-all-done.1.x1_ref = bf16[16,392,128]{2,1,0:T(8,128)(2,1)S(1)} async-done(((bf16[16,392,128]{2,1,0:T(8,128)(2,1)}), bf16[16,392,128]{2,1,0:T(8,128)(2,1)S(1)}, u32[]{:S(2)}, u32[]{:S(2)}) %all-to-all-start.1) | async-done | bytes 1605664 | tf_op jit(solution)/shard_map/all_to_all | solution.py:314
  62.0 3.8 %collective-permute-done.x2_ref = bf16[16,392,128]{2,1,0:T(8,128)(2,1)S(1)} collective-permute-done((bf16[16,392,128]{2,1,0:T(8,128)(2,1)}, bf16[16,392,128]{2,1,0:T(8,128)(2,1)S(1)}, u32[]{:S(2)}, u32[]{:S(2)}) %collective-permute-start) | collective-permute-done | bytes 1605664 | tf_op jit(solution)/shard_map/ppermute | solution.py:317
  65.8 4.4 %partial_grams.1 = (f32[264,128]{1,0:T(8,128)}, f32[264,128]{1,0:T(8,128)}, f32[264,128]{1,0:T(8,128)}, f32[264,128]{1,0:T(8,128)S(1)}) custom-call(s32[3]{0:T(128)S(1)} %pad_add_fusion.pos_ref, f32[2,128,128]{2,1,0:T(8,128)S(1)} %get-tuple-element.8.d0_ref, f32[8,128]{1,0:T(8,128)S(1)} %get-tuple-element.9.level_ref, ...), custom_call_target="tpu_custom_call" | custom-call | flops 805306368 | bytes 4718592 | tf_op jit(solution)/shard_map/partial_grams/pallas_call | solution.py:204
  70.2 2.6 %collective-permute-start.1 = (f32[264,128]{1,0:T(8,128)}, f32[264,128]{1,0:T(8,128)S(1)}, u32[]{:S(2)}, u32[]{:S(2)}) collective-permute-start(f32[264,128]{1,0:T(8,128)} %get-tuple-element.10), channel_id=1, source_target_pairs={{0,18},{1,19},{2,50},{3,51},{4,22},{5,23},{6,54},{7,55},{8,26},{9,... | collective-permute-start | bytes 405512 | tf_op jit(solution)/shard_map/ppermute | solution.py:322
  72.8 5.1 %collective-permute-start.2 = (f32[264,128]{1,0:T(8,128)}, f32[264,128]{1,0:T(8,128)S(1)}, u32[]{:S(2)}, u32[]{:S(2)}) collective-permute-start(f32[264,128]{1,0:T(8,128)} %get-tuple-element.11), channel_id=1, source_target_pairs={{0,22},{1,23},{2,54},{3,55},{4,18},{5,19},{6,50},{7,51},{8,30},{9,... | collective-permute-start | bytes 405512 | tf_op jit(solution)/shard_map/ppermute | solution.py:322
  77.9 4.2 %collective-permute-start.3 = (f32[264,128]{1,0:T(8,128)}, f32[264,128]{1,0:T(8,128)S(1)}, u32[]{:S(2)}, u32[]{:S(2)}) collective-permute-start(f32[264,128]{1,0:T(8,128)} %get-tuple-element.12), channel_id=1, source_target_pairs={{0,50},{1,51},{2,18},{3,19},{4,54},{5,55},{6,22},{7,23},{8,58},{9,... | collective-permute-start | bytes 405512 | tf_op jit(solution)/shard_map/ppermute | solution.py:322
  82.2 0.0 collective-permute-start.4
  82.2 0.0 collective-permute-done.1.refs_0_
  82.2 9.6 %collective-permute-done.2.refs_1_ = f32[264,128]{1,0:T(8,128)S(1)} collective-permute-done((f32[264,128]{1,0:T(8,128)}, f32[264,128]{1,0:T(8,128)S(1)}, u32[]{:S(2)}, u32[]{:S(2)}) %collective-permute-start.2) | collective-permute-done | bytes 135200 | tf_op jit(solution)/shard_map/ppermute | solution.py:322
  91.8 1.1 %collective-permute-done.3.refs_2_ = f32[264,128]{1,0:T(8,128)S(1)} collective-permute-done((f32[264,128]{1,0:T(8,128)}, f32[264,128]{1,0:T(8,128)S(1)}, u32[]{:S(2)}, u32[]{:S(2)}) %collective-permute-start.3) | collective-permute-done | bytes 135200 | tf_op jit(solution)/shard_map/ppermute | solution.py:322
  92.9 1.3 %collective-permute-done.4.refs_3_ = f32[264,128]{1,0:T(8,128)S(1)} collective-permute-done((f32[264,128]{1,0:T(8,128)S(1)}, f32[264,128]{1,0:T(8,128)S(1)}, u32[]{:S(2)}, u32[]{:S(2)}) %collective-permute-start.4) | collective-permute-done | bytes 135200 | tf_op jit(solution)/shard_map/ppermute | solution.py:322
  94.2 6.6 %solved_blocks.1 = (f32[1,128,128]{2,1,0:T(8,128)}, f32[1,128,128]{2,1,0:T(8,128)}) custom-call(s32[1]{0:T(128)} %bitcast.last_ref, f32[264,128]{1,0:T(8,128)S(1)} %collective-permute-done.1.refs_0_, f32[264,128]{1,0:T(8,128)S(1)} %collective-permute-done.2.refs_1_, f32[264,128]{1,0:T(8,128)S(1)} %collective-permute-done.3.refs_2_, ...), custom_call_target="tpu_custom_call" | custom-call | flops 10000000 | bytes 786432 | tf_op jit(solution)/shard_map/solved_blocks/pallas_call | solution.py:292
Async XLA Ops:
  0.6 4.0 %copy-start.2 = (f32[2]{0:T(128)S(1)}, f32[2]{0:T(128)}, u32[]{:S(2)}) copy-start(f32[2]{0:T(128)} %damping_ref.3) | copy-start | bytes 28
  5.6 1.2 %copy-start.1 = (bf16[16,49,8,128]{3,2,1,0:T(8,128)(2,1)}, bf16[16,49,8,128]{3,2,1,0:T(8,128)(2,1)S(1)}, u32[]{:S(2)}) copy-start(bf16[16,49,8,128]{3,2,1,0:T(8,128)(2,1)S(1)} %sent_columns.2) | copy-start | bytes 4816900
  6.8 30.8 %all-to-all-start = ((bf16[16,392,128]{2,1,0:T(8,128)(2,1)}), bf16[16,392,128]{2,1,0:T(8,128)(2,1)}, u32[]{:S(2)}, u32[]{:S(2)}) async-start(bf16[16,392,128]{2,1,0:T(8,128)(2,1)} %bitcast.13), calls=%async_computation | async-start | bytes 3211264 | tf_op jit(solution)/shard_map/all_to_all | solution.py:314
  15.5 1.2 %copy-start = (bf16[16,49,8,128]{3,2,1,0:T(8,128)(2,1)}, bf16[16,49,8,128]{3,2,1,0:T(8,128)(2,1)S(1)}, u32[]{:S(2)}) copy-start(bf16[16,49,8,128]{3,2,1,0:T(8,128)(2,1)S(1)} %sent_columns.3) | copy-start | bytes 4816900
  37.6 24.4 %all-to-all-start.1 = ((bf16[16,392,128]{2,1,0:T(8,128)(2,1)}), bf16[16,392,128]{2,1,0:T(8,128)(2,1)S(1)}, u32[]{:S(2)}, u32[]{:S(2)}) async-start(bf16[16,392,128]{2,1,0:T(8,128)(2,1)} %bitcast.12), calls=%async_computation.1 | async-start | bytes 3211264 | tf_op jit(solution)/shard_map/all_to_all | solution.py:314
  41.7 24.1 %collective-permute-start = (bf16[16,392,128]{2,1,0:T(8,128)(2,1)}, bf16[16,392,128]{2,1,0:T(8,128)(2,1)S(1)}, u32[]{:S(2)}, u32[]{:S(2)}) collective-permute-start(bf16[16,392,128]{2,1,0:T(8,128)(2,1)} %all-to-all-done.x_ref.x0_ref), channel_id=1, source_target_pairs={{64,0},{65,1},{66,2},{67,3},{68,4},{69,5},{70,6},{71,7},{72,8},{73... | collective-permute-start | bytes 4816904 | tf_op jit(solution)/shard_map/ppermute | solution.py:317
  70.2 12.0 %collective-permute-start.1 = (f32[264,128]{1,0:T(8,128)}, f32[264,128]{1,0:T(8,128)S(1)}, u32[]{:S(2)}, u32[]{:S(2)}) collective-permute-start(f32[264,128]{1,0:T(8,128)} %get-tuple-element.10), channel_id=1, source_target_pairs={{0,18},{1,19},{2,50},{3,51},{4,22},{5,23},{6,54},{7,55},{8,26},{9,... | collective-permute-start | bytes 405512 | tf_op jit(solution)/shard_map/ppermute | solution.py:322
  72.8 19.0 %collective-permute-start.2 = (f32[264,128]{1,0:T(8,128)}, f32[264,128]{1,0:T(8,128)S(1)}, u32[]{:S(2)}, u32[]{:S(2)}) collective-permute-start(f32[264,128]{1,0:T(8,128)} %get-tuple-element.11), channel_id=1, source_target_pairs={{0,22},{1,23},{2,54},{3,55},{4,18},{5,19},{6,50},{7,51},{8,30},{9,... | collective-permute-start | bytes 405512 | tf_op jit(solution)/shard_map/ppermute | solution.py:322
  77.9 15.0 %collective-permute-start.3 = (f32[264,128]{1,0:T(8,128)}, f32[264,128]{1,0:T(8,128)S(1)}, u32[]{:S(2)}, u32[]{:S(2)}) collective-permute-start(f32[264,128]{1,0:T(8,128)} %get-tuple-element.12), channel_id=1, source_target_pairs={{0,50},{1,51},{2,18},{3,19},{4,54},{5,55},{6,22},{7,23},{8,58},{9,... | collective-permute-start | bytes 405512 | tf_op jit(solution)/shard_map/ppermute | solution.py:322
  82.2 12.1 %collective-permute-start.4 = (f32[264,128]{1,0:T(8,128)S(1)}, f32[264,128]{1,0:T(8,128)S(1)}, u32[]{:S(2)}, u32[]{:S(2)}) collective-permute-start(f32[264,128]{1,0:T(8,128)S(1)} %get-tuple-element.13), channel_id=1, source_target_pairs={{0,54},{1,55},{2,22},{3,23},{4,50},{5,51},{6,18},{7,19},{8,62},{9,... | collective-permute-start | bytes 405512 | tf_op jit(solution)/shard_map/ppermute | solution.py:322
